TPU v7x, 32 devices: a 4x4x1 block of a 4x4x8 slice. The times are simulated.
32 devices in a mesh: dp: 1 (over z), tp: 32 (over y, x, core).
Axes of the slice: x: 4, y: 4, z: 1, core: 2. Of those that a mesh axis runs over, the one named last changes fastest.
The devices are a block of a 4x4x8 slice.
Arguments:
- y_one: float32 [96, 32, 2048], P('dp')
- y_two: float32 [96, 32, 2048], P('dp')
- dy_one: float32 [96, 32, 2048], P('dp')
- dy_two: float32 [96, 32, 2048], P('dp')
- seq_lens: int32 [96], P('dp')
- w_query: bfloat16 [1, 2048, 32, 64], P(None, None, 'tp')
- w_key: bfloat16 [1, 2048, 32, 64], P(None, None, 'tp')
- w_value: bfloat16 [1, 2048, 32, 64], P(None, None, 'tp')
- w_out: bfloat16 [1, 32, 64, 2048], P(None, 'tp')
- w_up: bfloat16 [1, 2048, 8192], P(None, None, 'tp')
- w_down: bfloat16 [1, 8192, 2048], P(None, 'tp')
Outputs:
- output 1: float32 [96, 32, 2048], P('dp')
- output 2: float32 [96, 32, 2048], P('dp')
- output 3: float32 [96, 32, 2048], P('dp')
- output 4: float32 [96, 32, 2048], P('dp')
- output 5: float32 [1, 2048, 32, 64], P('dp', None, 'tp')
- output 6: float32 [1, 2048, 32, 64], P('dp', None, 'tp')
- output 7: float32 [1, 2048, 32, 64], P('dp', None, 'tp')
- output 8: float32 [1, 32, 64, 2048], P('dp', 'tp')
- output 9: float32 [1, 2048, 8192], P('dp', None, 'tp')
- output 10: float32 [1, 8192, 2048], P('dp', 'tp')
All inputs are finite; a program needn't handle non-finite values.
Results may differ from a plain program's by a relative error of at most 0.00909588.
Values are sent between devices in bfloat16 or wider.
A program may use at most 768 MiB of HBM per device.

v0:
```python
import jax
import jax.numpy as jnp
from jax import lax
from jax.sharding import PartitionSpec as P, NamedSharding

F32 = jnp.float32
BF16 = jnp.bfloat16
EPS = 1e-5
MASK_VALUE = -1e30


def rms_norm(x_val):
    inv_rms = lax.rsqrt(jnp.mean(x_val * x_val, axis=-1, keepdims=True) + EPS)
    return x_val * inv_rms, inv_rms


def rms_back(normed, inv_rms, grad_norm):
    return inv_rms * (grad_norm - normed * jnp.mean(grad_norm * normed, axis=-1, keepdims=True))


def visible_mask(seq_lens, seq_len):
    row_pos = lax.broadcasted_iota(jnp.int32, (seq_len, seq_len), 0)
    col_pos = lax.broadcasted_iota(jnp.int32, (seq_len, seq_len), 1)
    causal = (col_pos <= row_pos)[None, None, None]
    in_length = col_pos[None, None, None] < seq_lens[:, None, None, None, None]
    return causal & in_length


def block_back(carry, seq_lens, layer_w, all_reduce):
    y_one, y_two, dy_one, dy_two = carry
    w_query, w_key, w_value, w_out, w_up, w_down = layer_w
    n_batch, seq_len = y_one.shape[0], y_one.shape[1]
    n_heads, head_dim = w_query.shape[1], w_query.shape[2]
    kv_slots = w_key.shape[1]
    group_size = n_heads // kv_slots
    score_scale = head_dim ** -0.5

    norm_g, inv_g = rms_norm(y_one)
    norm_g_b = norm_g.astype(BF16)
    pre_act = jnp.einsum('bsd,df->bsf', norm_g_b, w_up, preferred_element_type=F32)
    act_val, gelu_back = jax.vjp(jax.nn.gelu, pre_act)
    act_b = act_val.astype(BF16)
    x_two = y_two - all_reduce(jnp.einsum('bsf,fd->bsd', act_b, w_down, preferred_element_type=F32))
    dy2_b = dy_two.astype(BF16)
    d_act = jnp.einsum('bsd,fd->bsf', dy2_b, w_down, preferred_element_type=F32)
    d_pre = gelu_back(d_act)[0].astype(BF16)
    dw_down = jnp.einsum('bsf,bsd->fd', act_b, dy2_b, preferred_element_type=F32)
    dw_up = jnp.einsum('bsd,bsf->df', norm_g_b, d_pre, preferred_element_type=F32)
    grad_norm_g = all_reduce(jnp.einsum('bsf,df->bsd', d_pre, w_up, preferred_element_type=F32))
    dy_one = dy_one + rms_back(norm_g, inv_g, grad_norm_g)

    norm_f, inv_f = rms_norm(x_two)
    norm_f_b = norm_f.astype(BF16)
    query_proj = jnp.einsum('bsd,dhe->bshe', norm_f_b, w_query, preferred_element_type=F32).astype(BF16)
    query_grp = query_proj.reshape(n_batch, seq_len, kv_slots, group_size, head_dim)
    key_proj = jnp.einsum('bsd,dge->bsge', norm_f_b, w_key, preferred_element_type=F32).astype(BF16)
    value_proj = jnp.einsum('bsd,dge->bsge', norm_f_b, w_value, preferred_element_type=F32).astype(BF16)
    scores = jnp.einsum('bigre,bjge->bgrij', query_grp, key_proj, preferred_element_type=F32) * score_scale
    scores = jnp.where(visible_mask(seq_lens, seq_len), scores, MASK_VALUE)
    attn_probs = jax.nn.softmax(scores, axis=-1)
    probs_b = attn_probs.astype(BF16)
    attn_out = jnp.einsum('bgrij,bjge->bigre', probs_b, value_proj, preferred_element_type=F32).astype(BF16)
    attn_out = attn_out.reshape(n_batch, seq_len, n_heads, head_dim)
    x_one = y_one - all_reduce(jnp.einsum('bihe,hed->bid', attn_out, w_out, preferred_element_type=F32))
    dy1_b = dy_one.astype(BF16)
    dw_out = jnp.einsum('bihe,bid->hed', attn_out, dy1_b, preferred_element_type=F32)
    d_attn = jnp.einsum('bid,hed->bihe', dy1_b, w_out, preferred_element_type=F32).astype(BF16)
    d_attn = d_attn.reshape(n_batch, seq_len, kv_slots, group_size, head_dim)
    d_value = jnp.einsum('bgrij,bigre->bjge', probs_b, d_attn, preferred_element_type=F32).astype(BF16)
    d_probs = jnp.einsum('bigre,bjge->bgrij', d_attn, value_proj, preferred_element_type=F32)
    d_scores = (attn_probs * (d_probs - jnp.sum(d_probs * attn_probs, axis=-1, keepdims=True)) * score_scale).astype(BF16)
    d_query = jnp.einsum('bgrij,bjge->bigre', d_scores, key_proj, preferred_element_type=F32).astype(BF16)
    d_query = d_query.reshape(n_batch, seq_len, n_heads, head_dim)
    d_key = jnp.einsum('bgrij,bigre->bjge', d_scores, query_grp, preferred_element_type=F32).astype(BF16)
    dw_query = jnp.einsum('bsd,bshe->dhe', norm_f_b, d_query, preferred_element_type=F32)
    dw_key = jnp.einsum('bsd,bsge->dge', norm_f_b, d_key, preferred_element_type=F32)
    dw_value = jnp.einsum('bsd,bsge->dge', norm_f_b, d_value, preferred_element_type=F32)
    grad_norm_f = all_reduce(jnp.einsum('bshe,dhe->bsd', d_query, w_query, preferred_element_type=F32)
                             + jnp.einsum('bsge,dge->bsd', d_key, w_key, preferred_element_type=F32)
                             + jnp.einsum('bsge,dge->bsd', d_value, w_value, preferred_element_type=F32))
    dx_two = dy_two + rms_back(norm_f, inv_f, grad_norm_f)
    return (x_one, x_two, dy_one, dx_two), (dw_query, dw_key, dw_value, dw_out, dw_up, dw_down)


def stack_grads(grads_by_layer):
    return tuple(jnp.stack([layer_grads[grad_pos] for layer_grads in grads_by_layer]) for grad_pos in range(6))


def tp_sum(partial_val):
    return lax.psum(partial_val, 'tp')


def solution(mesh):
    act_spec = P('dp', None, None)
    w_specs = (P(None, None, 'tp', None), P(None, None, 'tp', None), P(None, None, 'tp', None),
               P(None, 'tp', None, None), P(None, None, 'tp'), P(None, 'tp', None))
    g_specs = (P('dp', None, 'tp', None), P('dp', None, 'tp', None), P('dp', None, 'tp', None),
               P('dp', 'tp', None, None), P('dp', None, 'tp'), P('dp', 'tp', None))

    def local_fn(y_one, y_two, dy_one, dy_two, seq_lens, w_query, w_key, w_value, w_out, w_up, w_down):
        weights = (w_query, w_key, w_value, w_out, w_up, w_down)
        carry = (y_one, y_two, dy_one, dy_two)
        n_layers = w_query.shape[0]
        grads_by_layer = [None] * n_layers
        for layer_idx in reversed(range(n_layers)):
            layer_w = tuple(w_stack[layer_idx] for w_stack in weights)
            carry, grads_by_layer[layer_idx] = block_back(carry, seq_lens, layer_w, tp_sum)
        return carry + stack_grads(grads_by_layer)

    return jax.shard_map(local_fn, mesh=mesh,
                         in_specs=(act_spec,) * 4 + (P('dp'),) + w_specs,
                         out_specs=(act_spec,) * 4 + g_specs,
                         check_vma=False)
```

profile of v0, /device:TPU:97, one launch (start us, length us, event | category | flops | bytes accessed | tf_op | source)
XLA Modules:
  0.0 1007.9 jit_solution(18443499245198614309)
XLA Ops:
  7.3 9.5 multiply_reduce_fusion.3
  16.8 10.7 %fusion.9 = f32[96,32,256]{2,1,0:T(8,128)S(1)} fusion(f32[96,32,2048]{2,1,0:T(8,128)} %param.11, f32[96,32]{1,0:T(8,128)S(1)} %add_rsqrt_fusion.1, bf16[1,2048,256]{2,1,0:T(8,128)(2,1)S(1)} %copy-done.7), kind=kOutput, calls=%fused_computation.18 | convolution fusion | flops 3233808384 | bytes 29372416 | tf_op jit(solution)/shard_map/bsd,df->bsf/dot_general | solution.py:40
  27.6 10.9 %fusion.41 = f32[96,32,2048]{2,1,0:T(8,128)} fusion(bf16[1,256,2048]{2,1,0:T(8,128)(2,1)S(1)} %copy-done, f32[96,32,256]{2,1,0:T(8,128)S(1)} %fusion.9), kind=kOutput, calls=%fused_computation.60 | convolution fusion | flops 3228303360 | bytes 29360128 | tf_op jit(solution)/shard_map/bsf,fd->bsd/dot_general | solution.py:43
  38.5 13.5 %fusion.16 = bf16[96,32,256]{2,1,0:T(8,128)(2,1)S(1)} fusion(f32[96,32,256]{2,1,0:T(8,128)S(1)} %fusion.9, f32[96,32,2048]{2,1,0:T(8,128)} %param.14, bf16[1,256,2048]{2,1,0:T(8,128)(2,1)S(1)} %copy-done), kind=kOutput, calls=%fused_computation.27 | convolution fusion | flops 3243245568 | bytes 30932992 | tf_op jit(solution)/shard_map/bsd,fd->bsf/dot_general | solution.py:45
  52.0 1.1 copy-done.5
  53.2 10.8 %fusion.43 = f32[96,32,2048]{2,1,0:T(8,128)} fusion(bf16[96,32,256]{2,1,0:T(8,128)(2,1)S(1)} %fusion.16, bf16[1,2048,256]{2,1,0:T(8,128)(2,1)S(1)} %copy-done.7), kind=kOutput, calls=%fused_computation.62 | convolution fusion | flops 3221225472 | bytes 27787264 | tf_op jit(solution)/shard_map/bsf,df->bsd/dot_general | solution.py:49
  64.3 345.4 %all-reduce.7.cloned.1.call-done = (f32[96,32,2048]{2,1,0:T(8,128)}, f32[96,32,2048]{2,1,0:T(8,128)}) async-done(((f32[96,32,2048]{2,1,0:T(8,128)}, f32[96,32,2048]{2,1,0:T(8,128)}), (f32[96,32,2048]{2,1,0:T(8,128)}, f32[96,32,2048]{2,1,0:T(8,128)})) %all-reduce.7.cloned.1.call-update) | async-done | bytes 50331664 | tf_op jit(solution)/shard_map/psum | solution.py:90
  409.7 40.2 %multiply_reduce_fusion.2 = (f32[96,32]{1,0:T(8,128)S(1)}, f32[96,32,2048]{2,1,0:T(8,128)}, f32[96,32]{1,0:T(8,128)S(1)}) fusion(f32[96,32,2048]{2,1,0:T(8,128)} %param.12, f32[96,32,2048]{2,1,0:T(8,128)} %get-tuple-element.12, f32[96,32,2048]{2,1,0:T(8,128)} %get-tuple-element.13, f32[96,32,2048]{2,1,0:T(8,128)} %param.11, f32[96,32]{1,0:T(8,128)S(1)} %add_rsqrt_fusion.1), kind=kLoop, calls=%fused_computation.5 | loop fusion | flops 37742592 | bytes 125865984 | tf_op jit(solution)/shard_map/reduce_sum | solution.py:13
  450.0 9.3 multiply_convert_fusion
  459.3 3.4 convolution_convert_fusion
  462.7 3.4 convolution_convert_fusion.1
  466.2 3.4 convolution_convert_fusion.2
  469.6 42.4 %multiply_add_fusion.1 = f32[96,32,2048]{2,1,0:T(8,128)} fusion(f32[96,32,2048]{2,1,0:T(8,128)} %param.13, f32[96,32,2048]{2,1,0:T(8,128)} %get-tuple-element.13, f32[96,32,2048]{2,1,0:T(8,128)} %param.11, f32[96,32]{1,0:T(8,128)S(1)} %broadcast_multiply_fusion.1, f32[96,32]{1,0:T(8,128)S(1)} %add_rsqrt_fusion.1), kind=kLoop, calls=%fused_computation.3 | loop fusion | flops 31457280 | bytes 100687872 | tf_op jit(solution)/shard_map/add | solution.py:50
  512.1 10.0 fusion.31
  522.1 0.7 fusion.64
  524.3 0.6 fusion.26
  524.9 0.6 fusion.46
  526.4 10.7 %fusion.60 = f32[96,32,2048]{2,1,0:T(8,128)} fusion(bf16[96,32,64]{2,1,0:T(8,128)(2,1)S(1)} %fusion.36, bf16[1,1,64,2048]{3,2,1,0:T(8,128)(2,1)S(1)} %copy-done.8), kind=kOutput, calls=%fused_computation.79 | convolution fusion | flops 805306368 | bytes 25821184 | tf_op jit(solution)/shard_map/bihe,hed->bid/dot_general | solution.py:64
  537.1 10.0 fusion.53
  547.0 10.7 %fusion.56 = f32[96,32,2048]{2,1,0:T(8,128)} fusion(bf16[96,32,64]{2,1,0:T(8,128)(2,1)S(1)} %fusion.37, bf16[1,2048,1,64]{1,3,2,0:T(8,128)(2,1)S(1)} %copy-done.12), kind=kOutput, calls=%fused_computation.75 | convolution fusion | flops 805306368 | bytes 25821184 | tf_op jit(solution)/shard_map/bshe,dhe->bsd/dot_general | solution.py:78
  557.7 26.4 %add_add_fusion = f32[96,32,2048]{2,1,0:T(8,128)} fusion(f32[96,32,2048]{2,1,0:T(8,128)} %fusion.56, f32[96,32,2048]{2,1,0:T(8,128)} %fusion.53, bf16[96,32,64]{2,1,0:T(8,128)(2,1)S(1)} %fusion.39, bf16[1,2048,1,64]{1,3,2,0:T(8,128)(2,1)S(1)} %copy-done.13), kind=kOutput, calls=%fused_computation.2 | convolution fusion | flops 817889280 | bytes 76152832 | tf_op jit(solution)/shard_map/bsge,dge->bsd/dot_general | solution.py:80
  584.3 14.1 %fusion.17 = f32[1,256,2048]{2,1,0:T(8,128)} fusion(f32[96,32,2048]{2,1,0:T(8,128)} %param.14, f32[96,32,256]{2,1,0:T(8,128)} %copy-done.4), kind=kOutput, calls=%fused_computation.29 | convolution fusion | flops 3234594816 | bytes 30408704 | tf_op jit(solution)/shard_map/bsf,bsd->fd/dot_general | solution.py:47
  598.3 13.8 %fusion.20 = f32[1,2048,256]{2,1,0:T(8,128)} fusion(bf16[96,32,256]{2,1,0:T(8,128)(2,1)S(1)} %copy-done.6, f32[96,32,2048]{2,1,0:T(8,128)} %param.11, f32[96,32]{1,0:T(8,128)S(1)} %add_rsqrt_fusion.1), kind=kOutput, calls=%fused_computation.30 | convolution fusion | flops 3233808384 | bytes 28848128 | tf_op jit(solution)/shard_map/bsd,bsf->df/dot_general | solution.py:48
  612.2 7.9 convolution_bitcast_fusion
  620.0 7.9 convolution_bitcast_fusion.2
  627.9 3.4 convolution_bitcast_fusion.1
  631.3 11.3 %fusion.21 = f32[1,1,64,2048]{3,2,1,0:T(8,128)} fusion(bf16[96,32,64]{2,1,0:T(8,128)(2,1)S(1)} %fusion.36, f32[96,32,2048]{2,1,0:T(8,128)} %multiply_add_fusion.1), kind=kOutput, calls=%fused_computation.31 | convolution fusion | flops 811597824 | bytes 26083328 | tf_op jit(solution)/shard_map/bihe,bid->hed/dot_general | solution.py:66
  642.6 282.8 %all-reduce.5.cloned.1.call-done = (f32[96,32,2048]{2,1,0:T(8,128)}, f32[96,32,2048]{2,1,0:T(8,128)}) async-done(((f32[96,32,2048]{2,1,0:T(8,128)}, f32[96,32,2048]{2,1,0:T(8,128)}), (f32[96,32,2048]{2,1,0:T(8,128)}, f32[96,32,2048]{2,1,0:T(8,128)})) %all-reduce.5.cloned.1.call-update) | async-done | bytes 50331664 | tf_op jit(solution)/shard_map/psum | solution.py:90
  925.4 26.4 %sub.34 = f32[96,32,2048]{2,1,0:T(8,128)} subtract(f32[96,32,2048]{2,1,0:T(8,128)} %param.11, f32[96,32,2048]{2,1,0:T(8,128)} %get-tuple-element.10) | non-fusion elementwise | flops 6291456 | bytes 75497472 | tf_op jit(solution)/shard_map/sub | solution.py:64
  951.9 5.2 copy-done.3
  957.1 10.4 %multiply_reduce_fusion = f32[96,32]{1,0:T(8,128)S(1)} fusion(f32[96,32,2048]{2,1,0:T(8,128)S(1)} %copy-done.3, f32[96,32,2048]{2,1,0:T(8,128)} %get-tuple-element.15, f32[96,32]{1,0:T(8,128)S(1)} %copy-done.10), kind=kLoop, calls=%fused_computation.1 | loop fusion | flops 18871296 | bytes 50356224 | tf_op jit(solution)/shard_map/reduce_sum | solution.py:18
  967.5 33.1 %multiply_add_fusion = f32[96,32,2048]{2,1,0:T(8,128)} fusion(f32[96,32,2048]{2,1,0:T(8,128)} %param.14, f32[96,32,2048]{2,1,0:T(8,128)} %get-tuple-element.11, f32[96,32,2048]{2,1,0:T(8,128)} %get-tuple-element.15, f32[96,32]{1,0:T(8,128)S(1)} %broadcast_multiply_fusion, f32[96,32]{1,0:T(8,128)S(1)} %copy-done.10), kind=kLoop, calls=%fused_computation | loop fusion | flops 31457280 | bytes 100687872 | tf_op jit(solution)/shard_map/add | solution.py:81
  (49 shorter events, 2.9 us)
Async XLA Ops:
  7.2 20.4 %copy-start = (bf16[1,256,2048]{2,1,0:T(8,128)(2,1)S(1)}, bf16[1,256,2048]{2,1,0:T(8,128)(2,1)}, u32[]{:S(2)}) copy-start(bf16[1,256,2048]{2,1,0:T(8,128)(2,1)} %param.21) | copy-start | bytes 3145732
  7.2 9.6 copy-start.7
  7.2 402.5 %all-reduce.7.cloned.1.call-start = ((), (), s32[]{:S(2)}) async-start(), calls=%async_computation.1 | async-start | bytes 100663296 | tf_op jit(solution)/shard_map/psum | solution.py:90
  27.6 10.9 %copy-start.4 = (f32[96,32,256]{2,1,0:T(8,128)}, f32[96,32,256]{2,1,0:T(8,128)S(1)}, u32[]{:S(2)}) copy-start(f32[96,32,256]{2,1,0:T(8,128)S(1)} %fusion.9) | copy-start | bytes 9437188
  52.0 1.1 copy-start.5
  64.0 861.5 %all-reduce.5.cloned.1.call-start = ((), (), s32[]{:S(2)}) async-start(), calls=%async_computation | async-start | bytes 100663296 | tf_op jit(solution)/shard_map/psum | solution.py:90
  449.9 9.3 copy-start.9
  450.0 9.3 copy-start.12
  459.3 6.9 copy-start.2
  459.3 3.4 copy-start.11
  462.7 3.5 copy-start.13
  469.6 42.4 %copy-start.8 = (bf16[1,1,64,2048]{3,2,1,0:T(8,128)(2,1)S(1)}, bf16[1,1,64,2048]{3,2,1,0:T(8,128)(2,1)}, u32[]{:S(2)}) copy-start(bf16[1,1,64,2048]{3,2,1,0:T(8,128)(2,1)} %param.19) | copy-start | bytes 786436
  512.1 10.1 copy-start.14
  584.2 14.1 %copy-start.6 = (bf16[96,32,256]{2,1,0:T(8,128)(2,1)S(1)}, bf16[96,32,256]{2,1,0:T(8,128)(2,1)}, u32[]{:S(2)}) copy-start(bf16[96,32,256]{2,1,0:T(8,128)(2,1)} %copy-done.5) | copy-start | bytes 4718596
  612.2 15.7 %slice-start = ((s8[12582912]{0:T(1024)(128)(4,1)}), s8[4194304]{0:T(1024)(128)(4,1)S(1)}, s32[]{:S(2)}) async-start(s8[12582912]{0:T(1024)(128)(4,1)} %bitcast.138), calls=%async_computation.2 | async-start | bytes 8388608
  612.2 15.7 %slice-start.1 = ((s8[12582912]{0:T(1024)(128)(4,1)}), s8[4194304]{0:T(1024)(128)(4,1)S(1)}, s32[]{:S(2)}) async-start(s8[12582912]{0:T(1024)(128)(4,1)} %bitcast.138), calls=%async_computation.3 | async-start | bytes 8388608
  620.0 7.9 slice-start.2
  925.4 31.6 %copy-start.3 = (f32[96,32,2048]{2,1,0:T(8,128)S(1)}, f32[96,32,2048]{2,1,0:T(8,128)}, u32[]{:S(2)}) copy-start(f32[96,32,2048]{2,1,0:T(8,128)} %get-tuple-element.11) | copy-start | bytes 75497472
  925.4 31.6 %copy-start.10 = (f32[96,32]{1,0:T(8,128)S(1)}, f32[96,32]{1,0:T(8,128)}, u32[]{:S(2)}) copy-start(f32[96,32]{1,0:T(8,128)} %copy-done.9) | copy-start | bytes 36868
  967.5 33.1 %copy-start.1 = (bf16[1,256,2048]{2,1,0:T(8,128)(2,1)S(1)}, bf16[1,256,2048]{2,1,0:T(8,128)(2,1)}, u32[]{:S(2)}) copy-start(bf16[1,256,2048]{2,1,0:T(8,128)(2,1)} %param.21) | copy-start | bytes 3145732
Sparse Core Ops, SparseCore 0:
  64.1 345.5 all-reduce.6
  584.4 341.0 all-reduce.4
where the time goes:
time: 1020 us; the launch traced here: 1010 us
  waiting for transfers between devices  628 us (62%)
  matrix products  185 us (18%)
  other arithmetic  173 us (17%)
  between operations  14.8 us (1%)
    psum x2, waiting for transfers between devices, tp_sum(): return lax.psum(partial_val, 'tp')  628 us
    reduce_sum x2, other arithmetic, rms_norm(): inv_rms = lax.rsqrt(jnp.mean(x_val * x_val, axis=-1, keepdims=True) + EPS)  49.7 us
    add x1, other arithmetic, block_back(): dy_one = dy_one + rms_back(norm_g, inv_g, grad_norm_g)  42.4 us
    add x1, other arithmetic, block_back(): dx_two = dy_two + rms_back(norm_f, inv_f, grad_norm_f)  33.1 us
    dot_general x1, matrix products, block_back(): jnp.einsum('bsge,dge->bsd', d_value, w_value, preferred_element_type=F32)  26.4 us
    sub x1, other arithmetic, block_back(): y_one - all_reduce(jnp.einsum('bihe,hed->bid', attn_out, w_out, preferred...  26.4 us
  transfers between devices with their start and end apart: 2, of which 2 were waited for; matrix products, arithmetic and copies ran while one was open for 6% of the time, Pallas kernels for 0%

commit v1 on v0

v1 whole, which is shorter than its diff:
```python
import functools

import jax
import jax.numpy as jnp
from jax import lax
from jax.experimental import pallas as pl
from jax.experimental.pallas import tpu as pltpu
from jax.sharding import PartitionSpec as P

F32 = jnp.float32
BF16 = jnp.bfloat16
EPS = 1e-5
MASK_VALUE = -1e30
GELU_COEF = 0.044715
GELU_SCALE = (2.0 / jnp.pi) ** 0.5
VMEM_LIMIT = 60 * 1024 * 1024
N_CHUNKS = 2
NN = (((1,), (0,)), ((), ()))
NT = (((1,), (1,)), ((), ()))
TN = (((0,), (0,)), ((), ()))


def dot(lhs, rhs, dims=NN):
    return lax.dot_general(lhs, rhs, dims, preferred_element_type=F32)


def rms_norm(x_val):
    inv_rms = lax.rsqrt(jnp.mean(x_val * x_val, axis=-1, keepdims=True) + EPS)
    return x_val * inv_rms, inv_rms


def rms_back(normed, inv_rms, grad_norm):
    return inv_rms * (grad_norm - normed * jnp.mean(grad_norm * normed, axis=-1, keepdims=True))


def gelu_and_slope(x_val):
    tanh_val = jnp.tanh(GELU_SCALE * (x_val + GELU_COEF * (x_val * x_val * x_val)))
    cdf = 0.5 * (1.0 + tanh_val)
    inner_slope = GELU_SCALE * (1.0 + 3.0 * GELU_COEF * (x_val * x_val))
    return x_val * cdf, cdf + x_val * (0.5 * (1.0 - tanh_val * tanh_val) * inner_slope)


def ffn_kernel(has_acc, *refs):
    y_ref, dy_ref, up_ref, down_ref = refs[:4]
    refs = refs[4:]
    if has_acc:
        up_acc, down_acc = refs[:2]
        refs = refs[2:]
    branch_ref, dnorm_ref, dup_ref, ddown_ref, up_t, down_t = refs

    @pl.when(pl.program_id(0) == 0)
    def _():
        up_t[...] = up_ref[...].T
        down_t[...] = down_ref[...].T
        dup_ref[...] = up_acc[...] if has_acc else jnp.zeros_like(dup_ref)
        ddown_ref[...] = down_acc[...] if has_acc else jnp.zeros_like(ddown_ref)

    norm_b = rms_norm(y_ref[...])[0].astype(BF16)
    dy_b = dy_ref[...].astype(BF16)
    act_val, slope = gelu_and_slope(dot(norm_b, up_ref[...]))
    act_b = act_val.astype(BF16)
    branch_ref[...] = dot(act_b, down_ref[...])
    d_pre = (slope * dot(dy_b, down_t[...])).astype(BF16)
    dnorm_ref[...] = dot(d_pre, up_t[...]).astype(BF16)
    ddown_ref[...] += dot(act_b, dy_b, TN)
    dup_ref[...] += dot(d_pre, norm_b, TN)


def attn_kernel(n_seq_tok, head_dim, n_alias, has_acc, *refs):
    y1_ref, y2_ref, dy1_ref, g_ref, dg_ref, ok_ref, qkv_ref, out_ref = refs[:8]
    refs = refs[8 + n_alias:]
    if has_acc:
        qkv_acc, out_acc = refs[:2]
        refs = refs[2:]
    x2_ref, dy1_out, branch_ref, dnorm_ref, dqkv_ref, dout_ref, qkv_t, out_t = refs
    score_scale = head_dim ** -0.5

    @pl.when(pl.program_id(0) == 0)
    def _():
        qkv_t[...] = qkv_ref[...].T
        out_t[...] = out_ref[...].T
        dqkv_ref[...] = qkv_acc[...] if has_acc else jnp.zeros_like(dqkv_ref)
        dout_ref[...] = out_acc[...] if has_acc else jnp.zeros_like(dout_ref)

    x_two = y2_ref[...] - g_ref[...]
    x2_ref[...] = x_two
    norm_b = rms_norm(x_two)[0].astype(BF16)
    normed, inv_rms = rms_norm(y1_ref[...])
    dy_one = dy1_ref[...] + rms_back(normed, inv_rms, dg_ref[...].astype(F32))
    dy1_out[...] = dy_one
    dy_b = dy_one.astype(BF16)

    qkv = dot(norm_b, qkv_t[...]).astype(BF16)
    d_attn = dot(dy_b, out_t[...]).astype(BF16)
    n_tok = qkv.shape[0]
    width = ok_ref.shape[-1]
    row_pos = lax.broadcasted_iota(jnp.int32, (width, width), 0)
    col_pos = lax.broadcasted_iota(jnp.int32, (width, width), 1)
    causal = (col_pos <= row_pos) & (row_pos // n_seq_tok == col_pos // n_seq_tok)
    attn_parts, dqkv_parts = [], []
    for part in range(n_tok // width):
        rows = slice(part * width, (part + 1) * width)
        query = qkv[rows, :head_dim]
        key = qkv[rows, head_dim:2 * head_dim]
        value = qkv[rows, 2 * head_dim:]
        d_out = d_attn[rows]
        visible = causal & (ok_ref[part] > 0.5)
        scores = jnp.where(visible, dot(query, key, NT) * score_scale, MASK_VALUE)
        expd = jnp.exp(scores - jnp.max(scores, axis=-1, keepdims=True))
        probs = expd / jnp.sum(expd, axis=-1, keepdims=True)
        probs_b = probs.astype(BF16)
        attn_parts.append(dot(probs_b, value).astype(BF16))
        d_value = dot(probs_b, d_out, TN).astype(BF16)
        d_probs = dot(d_out, value, NT)
        row_sum = jnp.sum(d_probs * probs, axis=-1, keepdims=True)
        d_scores = (probs * (d_probs - row_sum) * score_scale).astype(BF16)
        d_query = dot(d_scores, key).astype(BF16)
        d_key = dot(d_scores, query, TN).astype(BF16)
        dqkv_parts.append(jnp.concatenate([d_query, d_key, d_value], axis=1))
    attn = jnp.concatenate(attn_parts, axis=0)
    dqkv = jnp.concatenate(dqkv_parts, axis=0)
    branch_ref[...] = dot(attn, out_ref[...]).astype(BF16)
    dnorm_ref[...] = dot(dqkv, qkv_ref[...]).astype(BF16)
    dout_ref[...] += dot(attn, dy_b, TN)
    dqkv_ref[...] += dot(dqkv, norm_b, TN)


def widen_kernel(n_alias, *refs):
    x1_in, dx2_in = refs[:2]
    x1_ref, dx2_ref = refs[2 + n_alias:]
    x1_ref[...] = x1_in[...].astype(F32)
    dx2_ref[...] = dx2_in[...].astype(F32)


def tile_of(n_tok, want):
    tile = want
    while n_tok % tile:
        tile //= 2
    return tile


def shape_of(shape, dtype=F32):
    return jax.ShapeDtypeStruct(shape, dtype)


def params():
    return pltpu.CompilerParams(dimension_semantics=('arbitrary',), vmem_limit_bytes=VMEM_LIMIT)


def whole(arr):
    return pl.BlockSpec(arr.shape, lambda i: (0,) * len(arr.shape))


ANY = pl.BlockSpec(memory_space=pl.ANY)


def run_ffn(start, n_tok, y_one, dy_two, w_up, w_down, acc):
    width, cols = y_one.shape[1], w_up.shape[1]
    tile = tile_of(n_tok, 512)
    off = start // tile
    far = pl.BlockSpec((tile, width), lambda i: (off + i, 0))
    near = pl.BlockSpec((tile, width), lambda i: (i, 0))
    grad = pl.BlockSpec((cols, width), lambda i: (0, 0))
    return pl.pallas_call(
        functools.partial(ffn_kernel, acc is not None),
        grid=(n_tok // tile,),
        in_specs=[far, far, whole(w_up), whole(w_down)] + [grad] * (0 if acc is None else 2),
        out_specs=[near, near, grad, grad],
        out_shape=[shape_of((n_tok, width)), shape_of((n_tok, width), BF16)] + [shape_of((cols, width))] * 2,
        scratch_shapes=[pltpu.VMEM((cols, width), BF16), pltpu.VMEM((width, cols), BF16)],
        compiler_params=params(),
        cost_estimate=pl.CostEstimate(flops=12 * n_tok * width * cols, bytes_accessed=12 * n_tok * width,
                                      transcendentals=n_tok * cols),
        name='ffn',
    )(y_one, dy_two, w_up, w_down, *(acc or ()))


def run_attn(start, n_tok, seq_tok, head_dim, y_one, y_two, dy_one, g_sum, dg_sum, key_ok, w_qkv, w_out, prev, acc):
    n_all, width = y_one.shape
    tile = tile_of(n_tok, 256)
    off = start // tile
    far = pl.BlockSpec((tile, width), lambda i: (off + i, 0))
    near = pl.BlockSpec((tile, width), lambda i: (i, 0))
    group = key_ok.shape[-1]
    per_tile = tile // group
    ok_spec = pl.BlockSpec((per_tile, 1, group), lambda i: (off + i, 0, 0))
    n_alias = 0 if prev is None else 2
    grads = [whole(w_qkv), whole(w_out)]
    return pl.pallas_call(
        functools.partial(attn_kernel, seq_tok, head_dim, n_alias, acc is not None),
        grid=(n_tok // tile,),
        in_specs=[far, far, far, near, near, ok_spec] + grads + [ANY] * n_alias + (grads if acc is not None else []),
        out_specs=[far, far, near, near] + grads,
        out_shape=[shape_of((n_all, width))] * 2 + [shape_of((n_tok, width), BF16)] * 2
        + [shape_of(w_qkv.shape), shape_of(w_out.shape)],
        scratch_shapes=[pltpu.VMEM(w_qkv.shape[::-1], BF16), pltpu.VMEM(w_out.shape[::-1], BF16)],
        input_output_aliases={8 + k: k for k in range(n_alias)},
        compiler_params=params(),
        cost_estimate=pl.CostEstimate(flops=24 * n_tok * width * head_dim, bytes_accessed=28 * n_tok * width,
                                      transcendentals=n_tok * group),
        name='attn',
    )(y_one, y_two, dy_one, g_sum, dg_sum, key_ok, w_qkv, w_out, *(prev or ()), *(acc or ()))


def run_widen(start, n_all, x_one, dx_two, prev):
    n_tok, width = x_one.shape
    tile = tile_of(n_tok, 256)
    off = start // tile
    far = pl.BlockSpec((tile, width), lambda i: (off + i, 0))
    near = pl.BlockSpec((tile, width), lambda i: (i, 0))
    n_alias = 0 if prev is None else 2
    return pl.pallas_call(
        functools.partial(widen_kernel, n_alias),
        grid=(n_tok // tile,),
        in_specs=[near, near] + [ANY] * n_alias,
        out_specs=[far, far],
        out_shape=[shape_of((n_all, width))] * 2,
        input_output_aliases={2 + k: k for k in range(n_alias)},
        compiler_params=params(),
        cost_estimate=pl.CostEstimate(flops=16 * n_tok * width, bytes_accessed=12 * n_tok * width, transcendentals=0),
        name='widen',
    )(x_one, dx_two, *(prev or ()))


def split_tokens(n_seq, seq_tok):
    parts = N_CHUNKS
    while n_seq % parts:
        parts -= 1
    step = n_seq // parts * seq_tok
    return [(k * step, step) for k in range(parts)]


def block_back(carry, seq_lens, layer_w):
    y_one, y_two, dy_one, dy_two = carry
    w_query, w_key, w_value, w_out, w_up, w_down = layer_w
    n_seq, seq_tok = y_one.shape[:2]
    head_dim = w_query.shape[2]
    act_shape = y_one.shape
    y_one, y_two, dy_one, dy_two = (a.reshape(-1, a.shape[-1]) for a in carry)
    w_qkv = jnp.concatenate([w[:, 0, :].T for w in (w_query, w_key, w_value)], axis=0)
    wo_flat = w_out[0]
    chunks = split_tokens(n_seq, seq_tok)
    group = tile_of(chunks[0][1], 128)
    key_pos = lax.broadcasted_iota(jnp.int32, (n_seq, seq_tok), 1)
    key_ok = (key_pos < seq_lens[:, None]).astype(F32).reshape(-1, 1, group)

    rank = lax.axis_index('tp')

    def reduce_all(val, earlier):
        if earlier is not None:
            val = lax.optimization_barrier((val, earlier))[0]
        return lax.psum(val, 'tp')

    def reduce_rows(val):
        return lax.psum_scatter(val, 'tp', scatter_dimension=0, tiled=True)

    def gather_rows(val):
        return lax.all_gather(val, 'tp', axis=0, tiled=True)

    acc, g_parts = None, []
    for start, n_tok in chunks:
        g_part, dg_part, *acc = run_ffn(start, n_tok, y_one, dy_two, w_up, w_down, acc)
        g_parts.append((g_part, dg_part))
    dw_up, dw_down = acc[0].T, acc[1]
    g_sums, sums = [], (None, None)
    for pair in g_parts:
        sums = tuple(map(reduce_all, pair, sums))
        g_sums.append(sums)
    acc, state, f_parts = None, None, []
    for (start, n_tok), sums in zip(chunks, g_sums):
        outs = run_attn(start, n_tok, seq_tok, head_dim, y_one, y_two, dy_one, *sums, key_ok, w_qkv, wo_flat, state, acc)
        state, acc = outs[:2], outs[4:]
        f_parts.append(outs[2:4])
    x_two, dy_one_new = state
    dw_qkv, dw_out = acc
    state = None
    for (start, n_tok), parts in zip(chunks, f_parts):
        f_rows, df_rows = (reduce_rows(part).astype(F32) for part in parts)
        n_rows = f_rows.shape[0]
        y1_rows, x2_rows, dy2_rows = (lax.dynamic_slice_in_dim(arr, start + rank * n_rows, n_rows, 0)
                                      for arr in (y_one, x_two, dy_two))
        dx2_rows = dy2_rows + rms_back(*rms_norm(x2_rows), df_rows)
        ends = gather_rows((y1_rows - f_rows).astype(BF16)), gather_rows(dx2_rows.astype(BF16))
        state = run_widen(start, y_one.shape[0], *ends, state)
    x_one, dx_two = state
    dw_heads = [dw_qkv[k * head_dim:(k + 1) * head_dim].T[:, None, :] for k in range(3)]
    carry = tuple(a.reshape(act_shape) for a in (x_one, x_two, dy_one_new, dx_two))
    return carry, (*dw_heads, dw_out[None], dw_up, dw_down)


def stack_grads(grads_by_layer):
    return tuple(jnp.stack([layer_grads[grad_pos] for layer_grads in grads_by_layer]) for grad_pos in range(6))


def solution(mesh):
    act_spec = P('dp', None, None)
    w_specs = (P(None, None, 'tp', None), P(None, None, 'tp', None), P(None, None, 'tp', None),
               P(None, 'tp', None, None), P(None, None, 'tp'), P(None, 'tp', None))
    g_specs = (P('dp', None, 'tp', None), P('dp', None, 'tp', None), P('dp', None, 'tp', None),
               P('dp', 'tp', None, None), P('dp', None, 'tp'), P('dp', 'tp', None))

    def local_fn(y_one, y_two, dy_one, dy_two, seq_lens, w_query, w_key, w_value, w_out, w_up, w_down):
        weights = (w_query, w_key, w_value, w_out, w_up, w_down)
        carry = (y_one, y_two, dy_one, dy_two)
        n_layers = w_query.shape[0]
        grads_by_layer = [None] * n_layers
        for layer_idx in reversed(range(n_layers)):
            layer_w = tuple(w_stack[layer_idx] for w_stack in weights)
            carry, grads_by_layer[layer_idx] = block_back(carry, seq_lens, layer_w)
        return carry + stack_grads(grads_by_layer)

    return jax.shard_map(local_fn, mesh=mesh,
                         in_specs=(act_spec,) * 4 + (P('dp'),) + w_specs,
                         out_specs=(act_spec,) * 4 + g_specs,
                         check_vma=False)
```

time: 1020 us -> 1020 us (level); the launches traced: 1010 us -> 1020 us
  waiting for transfers between devices: 628 us -> 855 us
  matrix products: 185 us -> 0 us
  other arithmetic: 173 us -> 8.9 us
  Pallas kernels: 0 us -> 139 us
    reduce_scatter x0 -> x4, waiting for transfers between devices: none -> 286 us  [reduce_rows(): return lax.psum_scatter(val, 'tp', scatter_dimension=0, tiled=True)]
    psum x2 -> x4, waiting for transfers between devices: 628 us -> 407 us  [reduce_all(): return lax.psum(val, 'tp')]
    dot_general x24 -> x0, matrix products: 185 us -> none  [the longest x1 26.4 us: block_back(): jnp.einsum('bsge,dge->bsd', d_value, w_value, preferred_element_type=F32)]
    all_gather x0 -> x4, waiting for transfers between devices: none -> 159 us  [gather_rows(): return lax.all_gather(val, 'tp', axis=0, tiled=True)]
    pallas_call x0 -> x6, Pallas kernels: none -> 139 us  [the longest x2 68.8 us: run_attn(): pl.pallas_call(functools.partial(attn_kernel, seq_tok, head_dim, n_alias,...]
    add x2 -> x0, other arithmetic: 75.5 us -> none  [the longest x1 42.4 us: block_back(): dy_one = dy_one + rms_back(norm_g, inv_g, grad_norm_g)]
    reduce_sum x2 -> x1, other arithmetic: 49.7 us -> 1.28 us  [rms_norm(): inv_rms = lax.rsqrt(jnp.mean(x_val * x_val, axis=-1, keepdims=True) + EPS)]
    sub x1 -> x0, other arithmetic: 26.4 us -> none  [block_back(): y_one - all_reduce(jnp.einsum('bihe,hed->bid', attn_out, w_out, preferred...]
  transfers between devices with their start and end apart: 2 -> 12, of which waited for: 2 -> 12; matrix products, arithmetic and copies ran while one was open for 6% -> 1% of each run, Pallas kernels for 0% -> 10%
where the time goes in v1:
time: 1020 us
  waiting for transfers between devices  855 us (84%)
  Pallas kernels  139 us (14%)
  between operations  14.3 us (1%)
    psum x4, waiting for transfers between devices, reduce_all(): return lax.psum(val, 'tp')  407 us
    reduce_scatter x4, waiting for transfers between devices, reduce_rows(): return lax.psum_scatter(val, 'tp', scatter_dimension=0, tiled=True)  286 us
    all_gather x4, waiting for transfers between devices, gather_rows(): return lax.all_gather(val, 'tp', axis=0, tiled=True)  159 us
    pallas_call x2, Pallas kernels, run_attn(): pl.pallas_call(functools.partial(attn_kernel, seq_tok, head_dim, n_alias,...  68.8 us
    pallas_call x2, Pallas kernels, run_ffn(): pl.pallas_call(functools.partial(ffn_kernel, acc is not None), grid=(n_to...  43.4 us
    pallas_call x2, Pallas kernels, run_widen(): pl.pallas_call(functools.partial(widen_kernel, n_alias), grid=(n_tok // t...  27.3 us
  transfers between devices with their start and end apart: 12, of which 12 were waited for; matrix products, arithmetic and copies ran while one was open for 1% of the time, Pallas kernels for 10%

profile of v1, /device:TPU:97, one launch (start us, length us, event | category | flops | bytes accessed | tf_op | source)
XLA Modules:
  0.0 1023.8 jit_solution(4495621291810660915)
XLA Ops:
  7.3 21.0 %ffn.2 = (f32[1536,2048]{1,0:T(8,128)}, bf16[1536,2048]{1,0:T(8,128)(2,1)}, f32[256,2048]{1,0:T(8,128)}, f32[256,2048]{1,0:T(8,128)}) custom-call(f32[3072,2048]{1,0:T(8,128)} %bitcast.37, f32[3072,2048]{1,0:T(8,128)} %bitcast.42, bf16[2048,256]{1,0:T(8,128)(2,1)} %bitcast.53, bf16[256,2048]{1,0:T(8,128)(2,1)} %bitcast.55), custom_call_target="tpu_custom_call" | custom-call | flops 9663676416 | bytes 37748736 | tf_op jit(solution)/shard_map/ffn/pallas_call | solution.py:164
  28.4 0.7 all-reduce.5.cloned.1.call-update
  29.2 22.3 %ffn.3 = (f32[1536,2048]{1,0:T(8,128)}, bf16[1536,2048]{1,0:T(8,128)(2,1)}, f32[256,2048]{1,0:T(8,128)}, f32[256,2048]{1,0:T(8,128)}) custom-call(f32[3072,2048]{1,0:T(8,128)} %bitcast.38, f32[3072,2048]{1,0:T(8,128)} %bitcast.43, bf16[2048,256]{1,0:T(8,128)(2,1)} %bitcast.54, bf16[256,2048]{1,0:T(8,128)(2,1)} %bitcast.56, ...), custom_call_target="tpu_custom_call" | custom-call | flops 9663676416 | bytes 37748736 | tf_op jit(solution)/shard_map/ffn/pallas_call | solution.py:164
  51.6 86.1 %all-reduce.9.cloned.1.call-done.refs_4_ = bf16[1536,2048]{1,0:T(8,128)(2,1)} async-done(((bf16[1536,2048]{1,0:T(8,128)(2,1)}), bf16[1536,2048]{1,0:T(8,128)(2,1)}) %all-reduce.9.cloned.1.call-update) | async-done | bytes 6291472 | tf_op jit(solution)/shard_map/psum | solution.py:252
  137.8 125.0 %all-reduce.5.cloned.1.call-done.refs_3_ = f32[1536,2048]{1,0:T(8,128)} async-done(((f32[1536,2048]{1,0:T(8,128)}), f32[1536,2048]{1,0:T(8,128)}) %all-reduce.5.cloned.1.call-update) | async-done | bytes 12582928 | tf_op jit(solution)/shard_map/psum | solution.py:252
  262.9 0.2 reduce-scatter.9.cloned.1.call-start
  263.8 0.6 compare_convert_fusion.refs_5_
  264.4 0.9 pad_maximum_fusion.refs_6_
  265.3 35.0 %attn.2 = (f32[3072,2048]{1,0:T(8,128)}, f32[3072,2048]{1,0:T(8,128)}, bf16[1536,2048]{1,0:T(8,128)(2,1)}, bf16[1536,2048]{1,0:T(8,128)(2,1)}, f32[192,2048]{1,0:T(8,128)}, /*index=5*/f32[64,2048]{1,0:T(8,128)}) custom-call(f32[3072,2048]{1,0:T(8,128)} %bitcast.39, f32[3072,2048]{1,0:T(8,128)} %bitcast.45, f32[3072,2048]{1,0:T(8,128)} %bitcast.47, ...), custom_call_target="tpu_custom_call" | custom-call | flops 4831838208 | bytes 88080384 | tf_op jit(solution)/shard_map/attn/pallas_call | solution.py:189
  300.4 70.6 %all-reduce.11.cloned.1.call-done.refs_4_ = bf16[1536,2048]{1,0:T(8,128)(2,1)} async-done(((bf16[1536,2048]{1,0:T(8,128)(2,1)}), bf16[1536,2048]{1,0:T(8,128)(2,1)}) %all-reduce.11.cloned.1.call-update) | async-done | bytes 6291472 | tf_op jit(solution)/shard_map/psum | solution.py:252
  371.1 125.0 %all-reduce.7.cloned.1.call-done.refs_3_ = f32[1536,2048]{1,0:T(8,128)} async-done(((f32[1536,2048]{1,0:T(8,128)}), f32[1536,2048]{1,0:T(8,128)}) %all-reduce.7.cloned.1.call-update) | async-done | bytes 12582928 | tf_op jit(solution)/shard_map/psum | solution.py:252
  496.1 33.8 %attn.3 = (f32[3072,2048]{1,0:T(8,128)}, f32[3072,2048]{1,0:T(8,128)}, bf16[1536,2048]{1,0:T(8,128)(2,1)}, bf16[1536,2048]{1,0:T(8,128)(2,1)}, f32[192,2048]{1,0:T(8,128)}, /*index=5*/f32[64,2048]{1,0:T(8,128)}) custom-call(f32[3072,2048]{1,0:T(8,128)} %bitcast.40, f32[3072,2048]{1,0:T(8,128)} %bitcast.46, ...), custom_call_target="tpu_custom_call", output_to_operand_aliasing={{0}: (8, {}), {1}: (9, {})} | custom-call | flops 4831838208 | bytes 88080384 | tf_op jit(solution)/shard_map/attn/pallas_call | solution.py:189
  530.0 0.7 reduce-scatter.11.cloned.1.call-update
  530.9 0.7 reduce-scatter.7.cloned.1.call-update
  531.7 44.9 %reduce-scatter.9.cloned.1.call-done = bf16[48,2048]{1,0:T(8,128)(2,1)} async-done(((bf16[1536,2048]{1,0:T(8,128)(2,1)}), bf16[48,2048]{1,0:T(8,128)(2,1)}) %reduce-scatter.9.cloned.1.call-update) | async-done | bytes 196624 | tf_op jit(solution)/shard_map/reduce_scatter | solution.py:255
  576.5 81.9 %reduce-scatter.5.cloned.1.call-done = bf16[48,2048]{1,0:T(8,128)(2,1)} async-done(((bf16[1536,2048]{1,0:T(8,128)(2,1)}), bf16[48,2048]{1,0:T(8,128)(2,1)}) %reduce-scatter.5.cloned.1.call-update) | async-done | bytes 196624 | tf_op jit(solution)/shard_map/reduce_scatter | solution.py:255
  658.4 2.1 subtract_convert_fusion
  660.6 1.3 multiply_reduce_fusion
  661.9 77.9 %reduce-scatter.11.cloned.1.call-done = bf16[48,2048]{1,0:T(8,128)(2,1)} async-done(((bf16[1536,2048]{1,0:T(8,128)(2,1)}), bf16[48,2048]{1,0:T(8,128)(2,1)}) %reduce-scatter.11.cloned.1.call-update) | async-done | bytes 196624 | tf_op jit(solution)/shard_map/reduce_scatter | solution.py:255
  739.8 81.4 %reduce-scatter.7.cloned.1.call-done = bf16[48,2048]{1,0:T(8,128)(2,1)} async-done(((bf16[1536,2048]{1,0:T(8,128)(2,1)}), bf16[48,2048]{1,0:T(8,128)(2,1)}) %reduce-scatter.7.cloned.1.call-update) | async-done | bytes 196624 | tf_op jit(solution)/shard_map/reduce_scatter | solution.py:255
  821.3 1.5 fusion.4
  822.8 2.4 fusion.7
  825.4 0.7 all-gather.5.cloned.1.call-update
  826.2 0.6 all-gather.7.cloned.1.call-update
  826.8 1.8 copy.26
  828.6 2.5 slice_bitcast_fusion
  831.1 38.0 %all-gather.9.cloned.1.call-done.refs_0_ = bf16[1536,2048]{1,0:T(8,128)(2,1)} async-done(((bf16[48,2048]{1,0:T(8,128)(2,1)}), bf16[1536,2048]{1,0:T(8,128)(2,1)}) %all-gather.9.cloned.1.call-update) | async-done | bytes 6291472 | tf_op jit(solution)/shard_map/all_gather | solution.py:258
  869.1 45.1 %all-gather.11.cloned.1.call-done.refs_1_ = bf16[1536,2048]{1,0:T(8,128)(2,1)} async-done(((bf16[48,2048]{1,0:T(8,128)(2,1)}), bf16[1536,2048]{1,0:T(8,128)(2,1)}) %all-gather.11.cloned.1.call-update) | async-done | bytes 6291472 | tf_op jit(solution)/shard_map/all_gather | solution.py:258
  914.1 13.6 %widen.2 = (f32[3072,2048]{1,0:T(8,128)}, f32[3072,2048]{1,0:T(8,128)}) custom-call(bf16[1536,2048]{1,0:T(8,128)(2,1)} %all-gather.9.cloned.1.call-done.refs_0_, bf16[1536,2048]{1,0:T(8,128)(2,1)} %all-gather.11.cloned.1.call-done.refs_1_), custom_call_target="tpu_custom_call" | custom-call | flops 50331648 | bytes 37748736 | tf_op jit(solution)/shard_map/widen/pallas_call | solution.py:212
  927.7 31.0 %all-gather.5.cloned.1.call-done.refs_0_ = bf16[1536,2048]{1,0:T(8,128)(2,1)} async-done(((bf16[48,2048]{1,0:T(8,128)(2,1)}), bf16[1536,2048]{1,0:T(8,128)(2,1)}) %all-gather.5.cloned.1.call-update) | async-done | bytes 6291472 | tf_op jit(solution)/shard_map/all_gather | solution.py:258
  958.8 44.5 %all-gather.7.cloned.1.call-done.refs_1_ = bf16[1536,2048]{1,0:T(8,128)(2,1)} async-done(((bf16[48,2048]{1,0:T(8,128)(2,1)}), bf16[1536,2048]{1,0:T(8,128)(2,1)}) %all-gather.7.cloned.1.call-update) | async-done | bytes 6291472 | tf_op jit(solution)/shard_map/all_gather | solution.py:258
  1003.3 13.6 %widen.3 = (f32[3072,2048]{1,0:T(8,128)}, f32[3072,2048]{1,0:T(8,128)}) custom-call(bf16[1536,2048]{1,0:T(8,128)(2,1)} %all-gather.5.cloned.1.call-done.refs_0_, bf16[1536,2048]{1,0:T(8,128)(2,1)} %all-gather.7.cloned.1.call-done.refs_1_, f32[3072,2048]{1,0:T(8,128)} %get-tuple-element.53.refs_2_, ...), custom_call_target="tpu_custom_call", output_to_operand_aliasing={{0}: (2, {}), {1}: (3, {})} | custom-call | flops 50331648 | bytes 37748736 | tf_op jit(solution)/shard_map/widen/pallas_call | solution.py:212
  (36 shorter events, 1.7 us)
Async XLA Ops:
  7.2 130.5 %all-reduce.9.cloned.1.call-start = ((), (), s32[]{:S(2)}) async-start(), calls=%async_computation.6 | async-start | bytes 12582912 | tf_op jit(solution)/shard_map/psum | solution.py:252
  28.4 234.5 %all-reduce.5.cloned.1.call-start = ((), (), s32[]{:S(2)}) async-start(), calls=%async_computation.4 | async-start | bytes 25165824 | tf_op jit(solution)/shard_map/psum | solution.py:252
  29.2 341.9 %all-reduce.11.cloned.1.call-start = ((), (), s32[]{:S(2)}) async-start(), calls=%async_computation.7 | async-start | bytes 12582912 | tf_op jit(solution)/shard_map/psum | solution.py:252
  137.7 358.4 %all-reduce.7.cloned.1.call-start = ((), (), s32[]{:S(2)}) async-start(), calls=%async_computation.5 | async-start | bytes 25165824 | tf_op jit(solution)/shard_map/psum | solution.py:252
  262.8 0.7 copy-start.4
  262.8 1.6 copy-start.1
  262.8 1.6 copy-start.2
  262.8 1.6 copy-start.3
  262.9 313.6 %reduce-scatter.9.cloned.1.call-start = ((), (), s32[]{:S(2)}) async-start(), calls=%async_computation.12 | async-start | bytes 6488064 | tf_op jit(solution)/shard_map/reduce_scatter | solution.py:255
  300.4 358.0 %reduce-scatter.5.cloned.1.call-start = ((), (), s32[]{:S(2)}) async-start(), calls=%async_computation.8 | async-start | bytes 6488064 | tf_op jit(solution)/shard_map/reduce_scatter | solution.py:255
  530.0 209.8 %reduce-scatter.11.cloned.1.call-start = ((), (), s32[]{:S(2)}) async-start(), calls=%async_computation.14 | async-start | bytes 6488064 | tf_op jit(solution)/shard_map/reduce_scatter | solution.py:255
  530.8 290.5 %reduce-scatter.7.cloned.1.call-start = ((), (), s32[]{:S(2)}) async-start(), calls=%async_computation.10 | async-start | bytes 6488064 | tf_op jit(solution)/shard_map/reduce_scatter | solution.py:255
  530.9 295.9 %copy-start = (f32[256,2048]{1,0:T(8,128)S(1)}, f32[256,2048]{1,0:T(8,128)}, u32[]{:S(2)}) copy-start(f32[256,2048]{1,0:T(8,128)} %get-tuple-element.60) | copy-start | bytes 6291460
  531.6 337.5 %all-gather.9.cloned.1.call-start = ((), (), s32[]{:S(2)}) async-start(), calls=%async_computation.13 | async-start | bytes 6488064 | tf_op jit(solution)/shard_map/all_gather | solution.py:258
  660.5 253.6 %all-gather.11.cloned.1.call-start = ((), (), s32[]{:S(2)}) async-start(), calls=%async_computation.15 | async-start | bytes 6488064 | tf_op jit(solution)/shard_map/all_gather | solution.py:258
  825.3 133.5 %all-gather.5.cloned.1.call-start = ((), (), s32[]{:S(2)}) async-start(), calls=%async_computation.9 | async-start | bytes 6488064 | tf_op jit(solution)/shard_map/all_gather | solution.py:258
  826.1 177.2 %all-gather.7.cloned.1.call-start = ((), (), s32[]{:S(2)}) async-start(), calls=%async_computation.11 | async-start | bytes 6488064 | tf_op jit(solution)/shard_map/all_gather | solution.py:258
Sparse Core Ops, SparseCore 0:
  28.5 109.1 all-reduce.8
  141.8 121.0 all-reduce.4
  266.3 104.7 all-reduce.10
  375.0 121.0 all-reduce.6
  500.1 76.3 reduce-scatter.8
  580.5 77.8 reduce-scatter.4
  662.0 77.8 reduce-scatter.10
  743.4 77.8 reduce-scatter.6
  823.9 45.1 all-gather.8
  871.6 42.5 all-gather.10
  916.2 42.5 all-gather.4
  960.7 42.5 all-gather.6

commit v2 on v1

v2 whole, which is shorter than its diff:
```python
import functools

import jax
import jax.numpy as jnp
from jax import lax
from jax.experimental import pallas as pl
from jax.experimental.pallas import tpu as pltpu
from jax.sharding import PartitionSpec as P

F32 = jnp.float32
BF16 = jnp.bfloat16
EPS = 1e-5
MASK_VALUE = -1e30
GELU_COEF = 0.044715
GELU_SCALE = (2.0 / jnp.pi) ** 0.5
VMEM_LIMIT = 60 * 1024 * 1024
LANES = 128
MESH = pl.DeviceIdType.MESH
NN = (((1,), (0,)), ((), ()))
NT = (((1,), (1,)), ((), ()))
TN = (((0,), (0,)), ((), ()))


def dot(lhs, rhs, dims=NN):
    return lax.dot_general(lhs, rhs, dims, preferred_element_type=F32)


def rms_norm(x_val):
    inv_rms = lax.rsqrt(jnp.mean(x_val * x_val, axis=-1, keepdims=True) + EPS)
    return x_val * inv_rms, inv_rms


def rms_back(normed, inv_rms, grad_norm):
    return inv_rms * (grad_norm - normed * jnp.mean(grad_norm * normed, axis=-1, keepdims=True))


def gelu_and_slope(x_val):
    tanh_val = jnp.tanh(GELU_SCALE * (x_val + GELU_COEF * (x_val * x_val * x_val)))
    cdf = 0.5 * (1.0 + tanh_val)
    inner_slope = GELU_SCALE * (1.0 + 3.0 * GELU_COEF * (x_val * x_val))
    return x_val * cdf, cdf + x_val * (0.5 * (1.0 - tanh_val * tanh_val) * inner_slope)


def ffn_kernel(y_ref, dy_ref, up_ref, down_ref, branch_ref, dnorm_ref, dup_ref, ddown_ref, up_t, down_t):
    @pl.when(pl.program_id(0) == 0)
    def _():
        up_t[...] = up_ref[...].T
        down_t[...] = down_ref[...].T
        dup_ref[...] = jnp.zeros_like(dup_ref)
        ddown_ref[...] = jnp.zeros_like(ddown_ref)

    norm_b = rms_norm(y_ref[...])[0].astype(BF16)
    dy_b = dy_ref[...].astype(BF16)
    act_val, slope = gelu_and_slope(dot(norm_b, up_ref[...]))
    act_b = act_val.astype(BF16)
    branch_ref[...] = dot(act_b, down_ref[...])
    d_pre = (slope * dot(dy_b, down_t[...])).astype(BF16)
    dnorm_ref[...] = dot(d_pre, up_t[...]).astype(BF16)
    ddown_ref[...] += dot(act_b, dy_b, TN)
    dup_ref[...] += dot(d_pre, norm_b, TN)


def attn_kernel(n_seq_tok, head_dim, nf_ref, dy_ref, ok_ref, qkv_ref, out_ref,
                x2_ref, dy1_ref, branch_ref, dnorm_ref, dqkv_ref, dout_ref, qkv_t, out_t):
    score_scale = head_dim ** -0.5
    width = dy_ref.shape[1]

    @pl.when(pl.program_id(0) == 0)
    def _():
        qkv_t[...] = qkv_ref[...].T
        out_t[...] = out_ref[...].T
        dqkv_ref[...] = jnp.zeros_like(dqkv_ref)
        dout_ref[...] = jnp.zeros_like(dout_ref)

    norm_b = nf_ref[:, :width]
    scales = nf_ref[:, width:].astype(F32)
    x2_ref[...] = norm_b.astype(F32) * (scales[:, :1] + scales[:, LANES // 2:LANES // 2 + 1])
    dy_b = dy_ref[...]
    dy1_ref[...] = dy_b.astype(F32)

    qkv = dot(norm_b, qkv_t[...]).astype(BF16)
    d_attn = dot(dy_b, out_t[...]).astype(BF16)
    n_tok = qkv.shape[0]
    group = ok_ref.shape[-1]
    row_pos = lax.broadcasted_iota(jnp.int32, (group, group), 0)
    col_pos = lax.broadcasted_iota(jnp.int32, (group, group), 1)
    causal = (col_pos <= row_pos) & (row_pos // n_seq_tok == col_pos // n_seq_tok)
    attn_parts, dqkv_parts = [], []
    for part in range(n_tok // group):
        rows = slice(part * group, (part + 1) * group)
        query = qkv[rows, :head_dim]
        key = qkv[rows, head_dim:2 * head_dim]
        value = qkv[rows, 2 * head_dim:]
        d_out = d_attn[rows]
        visible = causal & (ok_ref[part] > 0.5)
        scores = jnp.where(visible, dot(query, key, NT) * score_scale, MASK_VALUE)
        expd = jnp.exp(scores - jnp.max(scores, axis=-1, keepdims=True))
        probs = expd / jnp.sum(expd, axis=-1, keepdims=True)
        probs_b = probs.astype(BF16)
        attn_parts.append(dot(probs_b, value).astype(BF16))
        d_value = dot(probs_b, d_out, TN).astype(BF16)
        d_probs = dot(d_out, value, NT)
        row_sum = jnp.sum(d_probs * probs, axis=-1, keepdims=True)
        d_scores = (probs * (d_probs - row_sum) * score_scale).astype(BF16)
        d_query = dot(d_scores, key).astype(BF16)
        d_key = dot(d_scores, query, TN).astype(BF16)
        dqkv_parts.append(jnp.concatenate([d_query, d_key, d_value], axis=1))
    attn = jnp.concatenate(attn_parts, axis=0)
    dqkv = jnp.concatenate(dqkv_parts, axis=0)
    branch_ref[...] = dot(attn, out_ref[...]).astype(BF16)
    dnorm_ref[...] = dot(dqkv, qkv_ref[...]).astype(BF16)
    dout_ref[...] += dot(attn, dy_b, TN)
    dqkv_ref[...] += dot(dqkv, norm_b, TN)


def widen_kernel(x1_in, dx2_in, x1_ref, dx2_ref):
    x1_ref[...] = x1_in[...].astype(F32)
    dx2_ref[...] = dx2_in[...].astype(F32)


def store_x2(total, rows, out, x2_out, at):
    x_two = rows['y_two'][at] - total[at]
    x2_out[at] = x_two
    normed, inv_rms = rms_norm(x_two)
    width = normed.shape[1]
    scale = jnp.broadcast_to(1.0 / inv_rms, (normed.shape[0], LANES))
    high = scale.astype(BF16).astype(F32)
    lane = lax.broadcasted_iota(jnp.int32, scale.shape, 1)
    out[at[0], :width] = normed.astype(BF16)
    out[at[0], width:] = jnp.where(lane < LANES // 2, high, scale - high).astype(BF16)


def store_dy1(total, rows, out, x2_out, at):
    out[at] = (rows['dy_one'][at] + rms_back(*rms_norm(rows['y_one'][at]), total[at])).astype(BF16)


def store_x1(total, rows, out, x2_out, at):
    out[at] = (rows['y_one'][at] - total[at]).astype(BF16)


def store_dx2(total, rows, out, x2_out, at):
    out[at] = (rows['dy_two'][at] + rms_back(*rms_norm(rows['x_two'][at]), total[at])).astype(BF16)


def exchange_kernel(side, row_names, stores, keeps_x2, *refs):
    n_row = len(row_names)
    parts, row_refs, refs = refs[:2], refs[2:2 + n_row], refs[2 + n_row:]
    outs, refs = refs[:2], refs[2:]
    x2_out = None
    if keeps_x2:
        x2_out, refs = refs[0], refs[1:]
    half, own, slot_a, slot_b, total, sent = (refs[2 * i:2 * i + 2] for i in range(6))
    refs = refs[12:]
    row_bufs, refs = dict(zip(row_names, refs[:n_row])), refs[n_row:]
    (pair_send, pair_recv, own_sem, a_send, a_recv, b_send, b_recv, row_sem, out_sem,
     c_send, c_recv, d_send, d_recv, e_send, e_recv) = refs
    steps = side - 1
    n_rows, width = total[0].shape
    quarter = width // 4

    me = lax.axis_index('tp')
    core = me % 2
    pos = {'x': (me // 2) % side, 'y': me // (2 * side)}
    partner = me + 1 - 2 * core
    other = {'x': 'y', 'y': 'x'}
    streams = (('x', 1), ('x', -1), ('y', 1), ('y', -1))

    def wrap(val):
        return (val + 2 * side) % side

    def device(axis, move):
        place = dict(pos)
        place[axis] = wrap(pos[axis] + move)
        return {'tp': (place['y'] * side + place['x']) * 2 + core}

    def cols(k, st):
        stop = (st + 1) * quarter if st < 3 else outs[k].shape[-1]
        return slice(st * quarter, stop)

    def line(ref, axis, block, *rest):
        return ref.at[(slice(None), block) + rest] if axis == 'x' else ref.at[(block, slice(None)) + rest]

    def remote(src, dst, send, recv, dev):
        return pltpu.make_async_remote_copy(src_ref=src, dst_ref=dst, send_sem=send, recv_sem=recv,
                                            device_id=dev, device_id_type=MESH)

    barrier = pltpu.get_barrier_semaphore()
    neighbours = [{'tp': partner}] + [device(axis, sign) for axis, sign in streams]
    for dev in neighbours:
        pl.semaphore_signal(barrier, inc=1, device_id=dev, device_id_type=MESH)

    row_copies = []
    for i, name in enumerate(row_names):
        src = row_refs[i] if name == 'x_two' else row_refs[i].at[pos['y'], pos['x'], core]
        row_copies.append(pltpu.make_async_copy(src, row_bufs[name], row_sem.at[i]))
        row_copies[-1].start()

    def own_copy(k, block):
        src = parts[k].at[block // side, block % side, core]
        return pltpu.make_async_copy(src, own[k].at[block % 2], own_sem.at[k, block % 2])

    for k in range(2):
        own_copy(k, 0).start()
    pl.semaphore_wait(barrier, len(neighbours))

    waits = []
    pair = {}
    for k in range(2):
        for row in range(side):
            pair[k, row] = remote(parts[k].at[row, :, 1 - core], half[k].at[row], pair_send.at[k, row],
                                  pair_recv.at[k, row], {'tp': partner})
            pair[k, row].start()
            waits.append(pair[k, row])

    def send_a(k, st, step):
        axis, sign = streams[st]
        if step == 0:
            src = line(half[k], axis, wrap(pos[axis] - sign), slice(None), slice(st * quarter, (st + 1) * quarter))
        else:
            src = slot_a[k].at[st, step - 1]
        copy = remote(src, slot_a[k].at[st, step], a_send.at[k, st, step], a_recv.at[k, st, step], device(axis, sign))
        copy.start()
        waits.append(copy)
        return copy

    def send_b(k, st, step):
        axis, sign = streams[st]
        axis = other[axis]
        if step == 0:
            src = slot_a[k].at[st, steps - 1, wrap(pos[axis] - sign)]
        else:
            src = slot_b[k].at[st, step - 1]
        copy = remote(src, slot_b[k].at[st, step], b_send.at[k, st, step], b_recv.at[k, st, step], device(axis, sign))
        copy.start()
        waits.append(copy)
        return copy

    going = {}
    for k in range(2):
        for block in range(side * side):
            row, col = block // side, block % side
            if block + 1 < side * side:
                own_copy(k, block + 1).start()
            if col == 0:
                pair[k, row].wait_recv()
            own_copy(k, block).wait()

            @pl.loop(0, n_rows // 16)
            def _(r, k=k, row=row, col=col, block=block):
                at = pl.ds(pl.multiple_of(r * 16, 16), 16)
                half[k][row, col, at] = (half[k][row, col, at].astype(F32)
                                         + own[k][block % 2, at].astype(F32)).astype(half[k].dtype)
        for st in range(4):
            going[k, st] = send_a(k, st, 0)

    for step in range(steps):
        for k in range(2):
            for st, (axis, sign) in enumerate(streams):
                going[k, st].wait_recv()
                mine = line(half[k], axis, wrap(pos[axis] - sign * (2 + step)), slice(None),
                            slice(st * quarter, (st + 1) * quarter))

                @pl.loop(0, side)
                def _(j, k=k, st=st, step=step, mine=mine):
                    slot_a[k][st, step, j] = (slot_a[k][st, step, j].astype(F32)
                                              + mine[j].astype(F32)).astype(slot_a[k].dtype)
                going[k, st] = send_a(k, st, step + 1) if step + 1 < steps else send_b(k, st, 0)

    for copy in row_copies:
        copy.wait()

    def gather_b(k, st, step):
        axis, sign = streams[st]
        axis = other[axis]
        at = dict(pos)
        at[axis] = wrap(pos[axis] - sign * step)
        block = outs[k].at[at['y'], at['x'], core, :, cols(k, st)]
        src = sent[k].at[:, cols(k, st)] if step == 0 else block
        copy = remote(src, block, c_send.at[k, st, step], c_recv.at[k, st, step], device(axis, sign))
        copy.start()
        waits.append(copy)
        return copy

    def gather_a(k, st, step):
        axis, sign = streams[st]
        group = line(outs[k], axis, wrap(pos[axis] - sign * step), core, slice(None), cols(k, st))
        if step < steps:
            copy = remote(group, group, d_send.at[k, st, step], d_recv.at[k, st, step], device(axis, sign))
            copy.start()
            waits.append(copy)
            going[k, st] = copy
        copy = remote(group, group, e_send.at[k, st, step], e_recv.at[k, st, step], {'tp': partner})
        copy.start()
        waits.append(copy)
        last.append(copy)

    last, out_copies = [], []
    for step in range(steps):
        for k in range(2):
            for st, (axis, sign) in enumerate(streams):
                going[k, st].wait_recv()
                mine = slot_a[k].at[st, steps - 1, wrap(pos[other[axis]] - sign * (2 + step))]
                if step + 1 < steps:
                    slot_b[k][st, step] = (slot_b[k][st, step].astype(F32) + mine[...].astype(F32)).astype(slot_b[k].dtype)
                    going[k, st] = send_b(k, st, step + 1)
                else:
                    total[k][:, st * quarter:(st + 1) * quarter] = slot_b[k][st, step].astype(F32) + mine[...].astype(F32)
            if step + 1 == steps:
                @pl.loop(0, n_rows // 16)
                def _(r, k=k):
                    at = (pl.ds(pl.multiple_of(r * 16, 16), 16), slice(0, width))
                    stores[k](total[k], row_bufs, sent[k], x2_out, at)
                out_copies.append(pltpu.make_async_copy(sent[k], outs[k].at[pos['y'], pos['x'], core], out_sem.at[k]))
                out_copies[-1].start()
                for st in range(4):
                    going[k, st] = gather_b(k, st, 0)

    for step in range(steps):
        for k in range(2):
            if step + 1 == steps:
                out_copies[k].wait()
            for st in range(4):
                going[k, st].wait_recv()
                if step + 1 < steps:
                    going[k, st] = gather_b(k, st, step + 1)
                else:
                    gather_a(k, st, 0)
    for step in range(steps):
        for k in range(2):
            for st in range(4):
                going[k, st].wait_recv()
                gather_a(k, st, step + 1)
    for copy in last:
        copy.wait_recv()
    for copy in waits:
        copy.wait_send()


def tile_of(n_tok, want):
    tile = want
    while n_tok % tile:
        tile //= 2
    return tile


def shape_of(shape, dtype=F32):
    return jax.ShapeDtypeStruct(shape, dtype)


def params():
    return pltpu.CompilerParams(dimension_semantics=('arbitrary',), vmem_limit_bytes=VMEM_LIMIT)


def whole(arr):
    return pl.BlockSpec(arr.shape, lambda i: (0,) * len(arr.shape))


ANY = pl.BlockSpec(memory_space=pl.ANY)


def run_ffn(y_one, dy_two, w_up, w_down):
    (n_tok, width), cols = y_one.shape, w_up.shape[1]
    tile = tile_of(n_tok, 512)
    rows = pl.BlockSpec((tile, width), lambda i: (i, 0))
    grad = pl.BlockSpec((cols, width), lambda i: (0, 0))
    return pl.pallas_call(
        ffn_kernel,
        grid=(n_tok // tile,),
        in_specs=[rows, rows, whole(w_up), whole(w_down)],
        out_specs=[rows, rows, grad, grad],
        out_shape=[shape_of((n_tok, width)), shape_of((n_tok, width), BF16)] + [shape_of((cols, width))] * 2,
        scratch_shapes=[pltpu.VMEM((cols, width), BF16), pltpu.VMEM((width, cols), BF16)],
        compiler_params=params(),
        cost_estimate=pl.CostEstimate(flops=12 * n_tok * width * cols, bytes_accessed=14 * n_tok * width,
                                      transcendentals=n_tok * cols),
        name='ffn',
    )(y_one, dy_two, w_up, w_down)


def run_attn(seq_tok, head_dim, norm_f, dy_one, key_ok, w_qkv, w_out):
    n_tok, width = dy_one.shape
    tile = tile_of(n_tok, 256)
    rows = pl.BlockSpec((tile, width), lambda i: (i, 0))
    group = key_ok.shape[-1]
    grads = [whole(w_qkv), whole(w_out)]
    return pl.pallas_call(
        functools.partial(attn_kernel, seq_tok, head_dim),
        grid=(n_tok // tile,),
        in_specs=[pl.BlockSpec((tile, norm_f.shape[1]), lambda i: (i, 0)), rows,
                  pl.BlockSpec((tile // group, 1, group), lambda i: (i, 0, 0))] + grads,
        out_specs=[rows, rows, rows, rows] + grads,
        out_shape=[shape_of((n_tok, width))] * 2 + [shape_of((n_tok, width), BF16)] * 2
        + [shape_of(w_qkv.shape), shape_of(w_out.shape)],
        scratch_shapes=[pltpu.VMEM(w_qkv.shape[::-1], BF16), pltpu.VMEM(w_out.shape[::-1], BF16)],
        compiler_params=params(),
        cost_estimate=pl.CostEstimate(flops=24 * n_tok * width * head_dim, bytes_accessed=16 * n_tok * width,
                                      transcendentals=n_tok * group),
        name='attn',
    )(norm_f, dy_one, key_ok, w_qkv, w_out)


def run_widen(x_one, dx_two):
    n_tok, width = x_one.shape
    tile = tile_of(n_tok, 256)
    rows = pl.BlockSpec((tile, width), lambda i: (i, 0))
    return pl.pallas_call(
        widen_kernel,
        grid=(n_tok // tile,),
        in_specs=[rows, rows],
        out_specs=[rows, rows],
        out_shape=[shape_of((n_tok, width))] * 2,
        compiler_params=params(),
        cost_estimate=pl.CostEstimate(flops=n_tok * width, bytes_accessed=12 * n_tok * width, transcendentals=0),
        name='widen',
    )(x_one, dx_two)


def run_exchange(n_dev, call_id, parts, row_arrays, stores, out_widths, keeps_x2, name):
    side = int(round((n_dev // 2) ** 0.5))
    n_tok, width = parts[0].shape
    n_rows = n_tok // n_dev
    quarter = width // 4

    def blocks(arr):
        return arr.reshape(side, side, 2, n_rows, arr.shape[1]) if arr.shape[0] == n_tok else arr

    outs = [shape_of((side, side, 2, n_rows, w), BF16) for w in out_widths]
    out_specs = [ANY] * 2
    if keeps_x2:
        outs.append(shape_of((n_rows, width)))
        out_specs.append(pl.BlockSpec(memory_space=pltpu.VMEM))
    kinds = [part.dtype for part in parts]
    scratch = [pltpu.VMEM((side, side, n_rows, width), kind) for kind in kinds]
    scratch += [pltpu.VMEM((2, n_rows, width), kind) for kind in kinds]
    scratch += [pltpu.VMEM((4, side - 1, side, n_rows, quarter), kind) for kind in kinds]
    scratch += [pltpu.VMEM((4, side - 1, n_rows, quarter), kind) for kind in kinds]
    scratch += [pltpu.VMEM((n_rows, width), F32)] * 2
    scratch += [pltpu.VMEM((n_rows, w), BF16) for w in out_widths]
    scratch += [pltpu.VMEM((n_rows, width), F32)] * len(row_arrays)
    dma = pltpu.SemaphoreType.DMA
    ring = dma((2, 4, side - 1))
    scratch += [dma((2, side))] * 2 + [dma((2, 2))] + [ring] * 4 + [dma((len(row_arrays),)), dma((2,))]
    scratch += [ring] * 4 + [dma((2, 4, side))] * 2
    gathered = pl.pallas_call(
        functools.partial(exchange_kernel, side, tuple(row_arrays), stores, keeps_x2),
        in_specs=[ANY] * (2 + len(row_arrays)),
        out_specs=out_specs,
        out_shape=outs,
        scratch_shapes=scratch,
        compiler_params=pltpu.CompilerParams(collective_id=call_id, has_side_effects=True,
                                             vmem_limit_bytes=VMEM_LIMIT),
        name=name,
    )(*map(blocks, parts), *map(blocks, row_arrays.values()))
    return [arr.reshape(-1, arr.shape[-1]) for arr in gathered]


def block_back(carry, seq_lens, layer_w, n_dev):
    w_query, w_key, w_value, w_out, w_up, w_down = layer_w
    act_shape = carry[0].shape
    n_seq, seq_tok, width = act_shape
    head_dim = w_query.shape[2]
    y_one, y_two, dy_one, dy_two = (a.reshape(-1, width) for a in carry)
    w_qkv = jnp.concatenate([w[:, 0, :].T for w in (w_query, w_key, w_value)], axis=0)
    group = tile_of(n_seq * seq_tok, 128)
    key_pos = lax.broadcasted_iota(jnp.int32, (n_seq, seq_tok), 1)
    key_ok = (key_pos < seq_lens[:, None]).astype(F32).reshape(-1, 1, group)

    g_part, dg_part, dw_up, dw_down = run_ffn(y_one, dy_two, w_up, w_down)
    norm_f, dy1_b, x2_rows = run_exchange(
        n_dev, 0, (g_part, dg_part), {'y_one': y_one, 'y_two': y_two, 'dy_one': dy_one},
        (store_x2, store_dy1), (width + LANES, width), True, 'exchange_g')
    x_two, dy_one, f_part, df_part, dw_qkv, dw_out = run_attn(seq_tok, head_dim, norm_f, dy1_b, key_ok, w_qkv, w_out[0])
    x1_b, dx2_b = run_exchange(
        n_dev, 1, (f_part, df_part), {'y_one': y_one, 'dy_two': dy_two, 'x_two': x2_rows},
        (store_x1, store_dx2), (width, width), False, 'exchange_f')
    x_one, dx_two = run_widen(x1_b, dx2_b)
    dw_heads = [dw_qkv[k * head_dim:(k + 1) * head_dim].T[:, None, :] for k in range(3)]
    carry = tuple(a.reshape(act_shape) for a in (x_one, x_two, dy_one, dx_two))
    return carry, (*dw_heads, dw_out[None], dw_up.T, dw_down)


def stack_grads(grads_by_layer):
    return tuple(jnp.stack([layer_grads[grad_pos] for layer_grads in grads_by_layer]) for grad_pos in range(6))


def solution(mesh):
    act_spec = P('dp', None, None)
    w_specs = (P(None, None, 'tp', None), P(None, None, 'tp', None), P(None, None, 'tp', None),
               P(None, 'tp', None, None), P(None, None, 'tp'), P(None, 'tp', None))
    g_specs = (P('dp', None, 'tp', None), P('dp', None, 'tp', None), P('dp', None, 'tp', None),
               P('dp', 'tp', None, None), P('dp', None, 'tp'), P('dp', 'tp', None))

    def local_fn(y_one, y_two, dy_one, dy_two, seq_lens, w_query, w_key, w_value, w_out, w_up, w_down):
        weights = (w_query, w_key, w_value, w_out, w_up, w_down)
        carry = (y_one, y_two, dy_one, dy_two)
        n_layers, n_dev = w_query.shape[0], mesh.shape['tp']
        grads_by_layer = [None] * n_layers
        for layer_idx in reversed(range(n_layers)):
            layer_w = tuple(w_stack[layer_idx] for w_stack in weights)
            carry, grads_by_layer[layer_idx] = block_back(carry, seq_lens, layer_w, n_dev)
        return carry + stack_grads(grads_by_layer)

    return jax.shard_map(local_fn, mesh=mesh,
                         in_specs=(act_spec,) * 4 + (P('dp'),) + w_specs,
                         out_specs=(act_spec,) * 4 + g_specs,
                         check_vma=False)
```

time: 1020 us -> 466 us (0.46)
  waiting for transfers between devices: 855 us -> 0 us
  Pallas kernels: 139 us -> 458 us
  between operations: 14.3 us -> 0.73 us
    psum x4 -> x0, waiting for transfers between devices: 407 us -> none  [reduce_all(): return lax.psum(val, 'tp')]
    pallas_call x6 -> x5, Pallas kernels: 139 us -> 458 us  [the longest x2 356 us: run_exchange(): pl.pallas_call(functools.partial(exchange_kernel, side, tuple(row_arrays)...]
    reduce_scatter x4 -> x0, waiting for transfers between devices: 286 us -> none  [reduce_rows(): return lax.psum_scatter(val, 'tp', scatter_dimension=0, tiled=True)]
    all_gather x4 -> x0, waiting for transfers between devices: 159 us -> none  [gather_rows(): return lax.all_gather(val, 'tp', axis=0, tiled=True)]
  transfers between devices with their start and end apart: 12 -> 0, of which waited for: 12 -> 0; matrix products, arithmetic and copies ran while one was open for 1% -> 0% of each run, Pallas kernels for 10% -> 0%
where the time goes in v2:
time: 466 us; the launch traced here: 465 us
  Pallas kernels  458 us (98%)
    pallas_call x2, Pallas kernels, run_exchange(): pl.pallas_call(functools.partial(exchange_kernel, side, tuple(row_arrays)...  356 us
    pallas_call x1, Pallas kernels, run_attn(): pl.pallas_call(functools.partial(attn_kernel, seq_tok, head_dim), grid=(n...  40 us
    pallas_call x1, Pallas kernels, run_ffn(): pl.pallas_call(ffn_kernel, grid=(n_tok // tile,), in_specs=[rows, rows, w...  35.4 us
    pallas_call x1, Pallas kernels, run_widen(): pl.pallas_call(widen_kernel, grid=(n_tok // tile,), in_specs=[rows, rows]...  26.8 us

profile of v2, /device:TPU:97, one launch (start us, length us, event | category | flops | bytes accessed | tf_op | source)
XLA Modules:
  0.0 465.3 jit_solution(15690172239039712319)
XLA Ops:
  0.7 0.1 iota.12
  0.7 0.7 lt.19
  1.5 0.1 lt.20
  1.6 0.1 lt.21
  1.7 0.6 compare_convert_fusion.ok_ref
  2.3 2.1 pad_maximum_fusion.qkv_ref
  4.4 35.4 %ffn.1 = (f32[3072,2048]{1,0:T(8,128)}, bf16[3072,2048]{1,0:T(8,128)(2,1)}, f32[256,2048]{1,0:T(8,128)}, f32[256,2048]{1,0:T(8,128)}) custom-call(f32[3072,2048]{1,0:T(8,128)} %bitcast.47, f32[3072,2048]{1,0:T(8,128)} %bitcast.53, bf16[2048,256]{1,0:T(8,128)(2,1)} %bitcast.68, bf16[256,2048]{1,0:T(8,128)(2,1)} %bitcast.69), custom_call_target="tpu_custom_call" | custom-call | flops 19327352832 | bytes 88080384 | tf_op jit(solution)/shard_map/ffn/pallas_call | solution.py:366
  39.8 0.0 copy-start
  39.8 202.1 %exchange_g.1 = (bf16[4,4,2,96,2176]{4,3,2,1,0:T(8,128)(2,1)}, bf16[4,4,2,96,2048]{4,3,2,1,0:T(8,128)(2,1)}, f32[96,2048]{1,0:T(8,128)}) custom-call(f32[4,4,2,96,2048]{4,3,2,1,0:T(8,128)} %bitcast.52, bf16[4,4,2,96,2048]{4,3,2,1,0:T(8,128)(2,1)} %bitcast.57, f32[4,4,2,96,2048]{4,3,2,1,0:T(8,128)} %bitcast.48, f32[4,4,2,96,2048]{4,3,2,1,0:T(8,128)} %bitcast.50, ...), custom_call_target="tpu_custom_call" | custom-call | tf_op jit(solution)/shard_map/exchange_g/pallas_call | solution.py:444
  241.8 0.0 copy-done
  241.8 1.8 copy.22
  243.7 40.0 %attn.1 = (f32[3072,2048]{1,0:T(8,128)}, f32[3072,2048]{1,0:T(8,128)}, bf16[3072,2048]{1,0:T(8,128)(2,1)}, bf16[3072,2048]{1,0:T(8,128)(2,1)}, f32[192,2048]{1,0:T(8,128)}, /*index=5*/f32[64,2048]{1,0:T(8,128)}) custom-call(bf16[3072,2176]{1,0:T(8,128)(2,1)} %bitcast.66, bf16[3072,2048]{1,0:T(8,128)(2,1)} %bitcast.67, ...), custom_call_target="tpu_custom_call" | custom-call | flops 9663676416 | bytes 100663296 | tf_op jit(solution)/shard_map/attn/pallas_call | solution.py:386
  283.7 0.0 copy-start.1
  283.7 153.5 %exchange_f.1 = (bf16[4,4,2,96,2048]{4,3,2,1,0:T(8,128)(2,1)}, bf16[4,4,2,96,2048]{4,3,2,1,0:T(8,128)(2,1)}) custom-call(bf16[4,4,2,96,2048]{4,3,2,1,0:T(8,128)(2,1)} %bitcast.55, bf16[4,4,2,96,2048]{4,3,2,1,0:T(8,128)(2,1)} %bitcast.56, f32[4,4,2,96,2048]{4,3,2,1,0:T(8,128)} %bitcast.49, f32[4,4,2,96,2048]{4,3,2,1,0:T(8,128)} %bitcast.54, ...), custom_call_target="tpu_custom_call" | custom-call | tf_op jit(solution)/shard_map/exchange_f/pallas_call | solution.py:444
  437.2 0.0 copy-done.1
  437.3 1.2 slice_bitcast_fusion
  438.4 26.8 %widen.1 = (f32[3072,2048]{1,0:T(8,128)}, f32[3072,2048]{1,0:T(8,128)}) custom-call(bf16[3072,2048]{1,0:T(8,128)(2,1)} %bitcast.58, bf16[3072,2048]{1,0:T(8,128)(2,1)} %bitcast.59), custom_call_target="tpu_custom_call" | custom-call | flops 6291456 | bytes 75497472 | tf_op jit(solution)/shard_map/widen/pallas_call | solution.py:406
  (1 shorter events, 0.0 us)
Async XLA Ops:
  39.8 202.1 %copy-start = (f32[256,2048]{1,0:T(8,128)S(1)}, f32[256,2048]{1,0:T(8,128)}, u32[]{:S(2)}) copy-start(f32[256,2048]{1,0:T(8,128)} %get-tuple-element.42) | copy-start | bytes 6291460
  283.7 153.5 %copy-start.1 = (f32[192,2048]{1,0:T(8,128)S(1)}, f32[192,2048]{1,0:T(8,128)}, u32[]{:S(2)}) copy-start(f32[192,2048]{1,0:T(8,128)} %get-tuple-element.40) | copy-start | bytes 4718596

commit v3 on v2

--- a/solution.py
+++ b/solution.py
@@ -60,17 +60,22 @@
     dup_ref[...] += dot(d_pre, norm_b, TN)
 
 
-def attn_kernel(n_seq_tok, head_dim, nf_ref, dy_ref, ok_ref, qkv_ref, out_ref,
-                x2_ref, dy1_ref, branch_ref, dnorm_ref, dqkv_ref, dout_ref, qkv_t, out_t):
+def attn_kernel(seq_tok, group, nf_ref, dy_ref, lens_ref, query_ref, key_ref, value_ref, out_ref, dup_ref,
+                x2_ref, dy1_ref, branch_ref, dnorm_ref, dq_ref, dk_ref, dv_ref, dout_ref, dup_t, qkv, qkv_t, out_t):
+    head_dim = query_ref.shape[0]
     score_scale = head_dim ** -0.5
-    width = dy_ref.shape[1]
+    n_tok, width = dy_ref.shape
+    grads = (dq_ref, dk_ref, dv_ref)
 
     @pl.when(pl.program_id(0) == 0)
     def _():
-        qkv_t[...] = qkv_ref[...].T
+        for k, w_ref in enumerate((query_ref, key_ref, value_ref)):
+            qkv[k * head_dim:(k + 1) * head_dim] = w_ref[...]
+            grads[k][...] = jnp.zeros_like(grads[k])
+        qkv_t[...] = qkv[...].T
         out_t[...] = out_ref[...].T
-        dqkv_ref[...] = jnp.zeros_like(dqkv_ref)
         dout_ref[...] = jnp.zeros_like(dout_ref)
+        dup_t[...] = dup_ref[...].T
 
     norm_b = nf_ref[:, :width]
     scales = nf_ref[:, width:].astype(F32)
@@ -78,21 +83,25 @@
     dy_b = dy_ref[...]
     dy1_ref[...] = dy_b.astype(F32)
 
-    qkv = dot(norm_b, qkv_t[...]).astype(BF16)
+    proj = dot(norm_b, qkv_t[...]).astype(BF16)
     d_attn = dot(dy_b, out_t[...]).astype(BF16)
-    n_tok = qkv.shape[0]
-    group = ok_ref.shape[-1]
     row_pos = lax.broadcasted_iota(jnp.int32, (group, group), 0)
     col_pos = lax.broadcasted_iota(jnp.int32, (group, group), 1)
-    causal = (col_pos <= row_pos) & (row_pos // n_seq_tok == col_pos // n_seq_tok)
+    causal = (col_pos <= row_pos) & (row_pos // seq_tok == col_pos // seq_tok)
+    lane = lax.broadcasted_iota(jnp.int32, (1, group), 1)
+    first_seq = pl.program_id(0) * (n_tok // seq_tok)
     attn_parts, dqkv_parts = [], []
     for part in range(n_tok // group):
         rows = slice(part * group, (part + 1) * group)
-        query = qkv[rows, :head_dim]
-        key = qkv[rows, head_dim:2 * head_dim]
-        value = qkv[rows, 2 * head_dim:]
+        query = proj[rows, :head_dim]
+        key = proj[rows, head_dim:2 * head_dim]
+        value = proj[rows, 2 * head_dim:]
         d_out = d_attn[rows]
-        visible = causal & (ok_ref[part] > 0.5)
+        limit = jnp.zeros_like(lane)
+        for seq in range(group // seq_tok):
+            seq_len = lens_ref[first_seq + part * (group // seq_tok) + seq]
+            limit = jnp.where(lane // seq_tok == seq, seq_len, limit)
+        visible = causal & (lane % seq_tok < limit)
         scores = jnp.where(visible, dot(query, key, NT) * score_scale, MASK_VALUE)
         expd = jnp.exp(scores - jnp.max(scores, axis=-1, keepdims=True))
         probs = expd / jnp.sum(expd, axis=-1, keepdims=True)
@@ -108,9 +117,11 @@
     attn = jnp.concatenate(attn_parts, axis=0)
     dqkv = jnp.concatenate(dqkv_parts, axis=0)
     branch_ref[...] = dot(attn, out_ref[...]).astype(BF16)
-    dnorm_ref[...] = dot(dqkv, qkv_ref[...]).astype(BF16)
+    dnorm_ref[...] = dot(dqkv, qkv[...]).astype(BF16)
     dout_ref[...] += dot(attn, dy_b, TN)
-    dqkv_ref[...] += dot(dqkv, norm_b, TN)
+    d_heads = dot(dqkv, norm_b, TN)
+    for k, grad in enumerate(grads):
+        grad[...] += d_heads[k * head_dim:(k + 1) * head_dim]
 
 
 def widen_kernel(x1_in, dx2_in, x1_ref, dx2_ref):
@@ -149,7 +160,7 @@
     x2_out = None
     if keeps_x2:
         x2_out, refs = refs[0], refs[1:]
-    half, own, slot_a, slot_b, total, sent = (refs[2 * i:2 * i + 2] for i in range(6))
+    paired, own, slot_a, slot_b, total, sent = (refs[2 * i:2 * i + 2] for i in range(6))
     refs = refs[12:]
     row_bufs, refs = dict(zip(row_names, refs[:n_row])), refs[n_row:]
     (pair_send, pair_recv, own_sem, a_send, a_recv, b_send, b_recv, row_sem, out_sem,
@@ -195,27 +206,34 @@
         row_copies.append(pltpu.make_async_copy(src, row_bufs[name], row_sem.at[i]))
         row_copies[-1].start()
 
-    def own_copy(k, block):
-        src = parts[k].at[block // side, block % side, core]
-        return pltpu.make_async_copy(src, own[k].at[block % 2], own_sem.at[k, block % 2])
+    def piece(k, st, turn, whose):
+        axis, sign = streams[st]
+        return line(parts[k], axis, wrap(pos[axis] - sign * (1 + turn)), whose, slice(None),
+                    slice(st * quarter, (st + 1) * quarter))
+
+    def own_copy(k, st, turn):
+        return pltpu.make_async_copy(piece(k, st, turn, core), own[k].at[st], own_sem.at[k, st])
 
     for k in range(2):
-        own_copy(k, 0).start()
+        for st in range(4):
+            own_copy(k, st, 0).start()
     pl.semaphore_wait(barrier, len(neighbours))
 
     waits = []
     pair = {}
-    for k in range(2):
-        for row in range(side):
-            pair[k, row] = remote(parts[k].at[row, :, 1 - core], half[k].at[row], pair_send.at[k, row],
-                                  pair_recv.at[k, row], {'tp': partner})
-            pair[k, row].start()
-            waits.append(pair[k, row])
+    for turn in range(side):
+        for k in range(2):
+            for st in range(4):
+                copy = remote(piece(k, st, turn, 1 - core), paired[k].at[st, turn], pair_send.at[k, st, turn],
+                              pair_recv.at[k, st, turn], {'tp': partner})
+                copy.start()
+                pair[k, st, turn] = copy
+                waits.append(copy)
 
     def send_a(k, st, step):
         axis, sign = streams[st]
         if step == 0:
-            src = line(half[k], axis, wrap(pos[axis] - sign), slice(None), slice(st * quarter, (st + 1) * quarter))
+            src = paired[k].at[st, 0]
         else:
             src = slot_a[k].at[st, step - 1]
         copy = remote(src, slot_a[k].at[st, step], a_send.at[k, st, step], a_recv.at[k, st, step], device(axis, sign))
@@ -236,35 +254,25 @@
         return copy
 
     going = {}
-    for k in range(2):
-        for block in range(side * side):
-            row, col = block // side, block % side
-            if block + 1 < side * side:
-                own_copy(k, block + 1).start()
-            if col == 0:
-                pair[k, row].wait_recv()
-            own_copy(k, block).wait()
-
-            @pl.loop(0, n_rows // 16)
-            def _(r, k=k, row=row, col=col, block=block):
-                at = pl.ds(pl.multiple_of(r * 16, 16), 16)
-                half[k][row, col, at] = (half[k][row, col, at].astype(F32)
-                                         + own[k][block % 2, at].astype(F32)).astype(half[k].dtype)
-        for st in range(4):
-            going[k, st] = send_a(k, st, 0)
-
-    for step in range(steps):
+    for turn in range(side):
         for k in range(2):
-            for st, (axis, sign) in enumerate(streams):
-                going[k, st].wait_recv()
-                mine = line(half[k], axis, wrap(pos[axis] - sign * (2 + step)), slice(None),
-                            slice(st * quarter, (st + 1) * quarter))
+            for st in range(4):
+                if turn:
+                    going[k, st].wait_recv()
+                pair[k, st, turn].wait_recv()
+                own_copy(k, st, turn).wait()
 
                 @pl.loop(0, side)
-                def _(j, k=k, st=st, step=step, mine=mine):
-                    slot_a[k][st, step, j] = (slot_a[k][st, step, j].astype(F32)
-                                              + mine[j].astype(F32)).astype(slot_a[k].dtype)
-                going[k, st] = send_a(k, st, step + 1) if step + 1 < steps else send_b(k, st, 0)
+                def _(j, k=k, st=st, turn=turn):
+                    mine = paired[k][st, turn, j].astype(F32) + own[k][st, j].astype(F32)
+                    if turn:
+                        slot_a[k][st, turn - 1, j] = (slot_a[k][st, turn - 1, j].astype(F32) + mine).astype(slot_a[k].dtype)
+                    else:
+                        paired[k][st, 0, j] = mine.astype(paired[k].dtype)
+
+                if turn < steps:
+                    own_copy(k, st, turn + 1).start()
+                going[k, st] = send_a(k, st, turn) if turn < steps else send_b(k, st, 0)
 
     for copy in row_copies:
         copy.wait()
@@ -377,31 +385,34 @@
     )(y_one, dy_two, w_up, w_down)
 
 
-def run_attn(seq_tok, head_dim, norm_f, dy_one, key_ok, w_qkv, w_out):
+def run_attn(seq_tok, norm_f, dy_one, seq_lens, w_heads, w_out, dw_up):
     n_tok, width = dy_one.shape
+    head_dim = w_out.shape[0]
     tile = tile_of(n_tok, 256)
+    group = tile_of(tile, 128)
     rows = pl.BlockSpec((tile, width), lambda i: (i, 0))
-    group = key_ok.shape[-1]
-    grads = [whole(w_qkv), whole(w_out)]
+    grads = [whole(w) for w in w_heads] + [whole(w_out)]
+    up_shape = dw_up.shape[::-1]
     return pl.pallas_call(
-        functools.partial(attn_kernel, seq_tok, head_dim),
+        functools.partial(attn_kernel, seq_tok, group),
         grid=(n_tok // tile,),
         in_specs=[pl.BlockSpec((tile, norm_f.shape[1]), lambda i: (i, 0)), rows,
-                  pl.BlockSpec((tile // group, 1, group), lambda i: (i, 0, 0))] + grads,
-        out_specs=[rows, rows, rows, rows] + grads,
+                  pl.BlockSpec(memory_space=pltpu.SMEM)] + grads + [whole(dw_up)],
+        out_specs=[rows, rows, rows, rows] + grads + [pl.BlockSpec(up_shape, lambda i: (0, 0))],
         out_shape=[shape_of((n_tok, width))] * 2 + [shape_of((n_tok, width), BF16)] * 2
-        + [shape_of(w_qkv.shape), shape_of(w_out.shape)],
-        scratch_shapes=[pltpu.VMEM(w_qkv.shape[::-1], BF16), pltpu.VMEM(w_out.shape[::-1], BF16)],
+        + [shape_of(w_out.shape)] * 4 + [shape_of(up_shape)],
+        scratch_shapes=[pltpu.VMEM((3 * head_dim, width), BF16), pltpu.VMEM((width, 3 * head_dim), BF16),
+                        pltpu.VMEM((width, head_dim), BF16)],
         compiler_params=params(),
         cost_estimate=pl.CostEstimate(flops=24 * n_tok * width * head_dim, bytes_accessed=16 * n_tok * width,
                                       transcendentals=n_tok * group),
         name='attn',
-    )(norm_f, dy_one, key_ok, w_qkv, w_out)
+    )(norm_f, dy_one, seq_lens, *w_heads, w_out, dw_up)
 
 
 def run_widen(x_one, dx_two):
     n_tok, width = x_one.shape
-    tile = tile_of(n_tok, 256)
+    tile = tile_of(n_tok, 384)
     rows = pl.BlockSpec((tile, width), lambda i: (i, 0))
     return pl.pallas_call(
         widen_kernel,
@@ -430,8 +441,8 @@
         outs.append(shape_of((n_rows, width)))
         out_specs.append(pl.BlockSpec(memory_space=pltpu.VMEM))
     kinds = [part.dtype for part in parts]
-    scratch = [pltpu.VMEM((side, side, n_rows, width), kind) for kind in kinds]
-    scratch += [pltpu.VMEM((2, n_rows, width), kind) for kind in kinds]
+    scratch = [pltpu.VMEM((4, side, side, n_rows, quarter), kind) for kind in kinds]
+    scratch += [pltpu.VMEM((4, side, n_rows, quarter), kind) for kind in kinds]
     scratch += [pltpu.VMEM((4, side - 1, side, n_rows, quarter), kind) for kind in kinds]
     scratch += [pltpu.VMEM((4, side - 1, n_rows, quarter), kind) for kind in kinds]
     scratch += [pltpu.VMEM((n_rows, width), F32)] * 2
@@ -439,7 +450,7 @@
     scratch += [pltpu.VMEM((n_rows, width), F32)] * len(row_arrays)
     dma = pltpu.SemaphoreType.DMA
     ring = dma((2, 4, side - 1))
-    scratch += [dma((2, side))] * 2 + [dma((2, 2))] + [ring] * 4 + [dma((len(row_arrays),)), dma((2,))]
+    scratch += [dma((2, 4, side))] * 2 + [dma((2, 4))] + [ring] * 4 + [dma((len(row_arrays),)), dma((2,))]
     scratch += [ring] * 4 + [dma((2, 4, side))] * 2
     gathered = pl.pallas_call(
         functools.partial(exchange_kernel, side, tuple(row_arrays), stores, keeps_x2),
@@ -457,26 +468,23 @@
 def block_back(carry, seq_lens, layer_w, n_dev):
     w_query, w_key, w_value, w_out, w_up, w_down = layer_w
     act_shape = carry[0].shape
-    n_seq, seq_tok, width = act_shape
-    head_dim = w_query.shape[2]
+    seq_tok, width = act_shape[1:]
     y_one, y_two, dy_one, dy_two = (a.reshape(-1, width) for a in carry)
-    w_qkv = jnp.concatenate([w[:, 0, :].T for w in (w_query, w_key, w_value)], axis=0)
-    group = tile_of(n_seq * seq_tok, 128)
-    key_pos = lax.broadcasted_iota(jnp.int32, (n_seq, seq_tok), 1)
-    key_ok = (key_pos < seq_lens[:, None]).astype(F32).reshape(-1, 1, group)
+    w_heads = [w[:, 0, :].T for w in (w_query, w_key, w_value)]
 
     g_part, dg_part, dw_up, dw_down = run_ffn(y_one, dy_two, w_up, w_down)
-    norm_f, dy1_b, x2_rows = run_exchange(
-        n_dev, 0, (g_part, dg_part), {'y_one': y_one, 'y_two': y_two, 'dy_one': dy_one},
-        (store_x2, store_dy1), (width + LANES, width), True, 'exchange_g')
-    x_two, dy_one, f_part, df_part, dw_qkv, dw_out = run_attn(seq_tok, head_dim, norm_f, dy1_b, key_ok, w_qkv, w_out[0])
+    dy1_b, norm_f, x2_rows = run_exchange(
+        n_dev, 0, (dg_part, g_part), {'y_one': y_one, 'y_two': y_two, 'dy_one': dy_one},
+        (store_dy1, store_x2), (width, width + LANES), True, 'exchange_g')
+    x_two, dy_one, f_part, df_part, *dw_heads, dw_out, dw_up = run_attn(
+        seq_tok, norm_f, dy1_b, seq_lens, w_heads, w_out[0], dw_up)
     x1_b, dx2_b = run_exchange(
         n_dev, 1, (f_part, df_part), {'y_one': y_one, 'dy_two': dy_two, 'x_two': x2_rows},
         (store_x1, store_dx2), (width, width), False, 'exchange_f')
     x_one, dx_two = run_widen(x1_b, dx2_b)
-    dw_heads = [dw_qkv[k * head_dim:(k + 1) * head_dim].T[:, None, :] for k in range(3)]
+    dw_heads = [dw.T[:, None, :] for dw in dw_heads]
     carry = tuple(a.reshape(act_shape) for a in (x_one, x_two, dy_one, dx_two))
-    return carry, (*dw_heads, dw_out[None], dw_up.T, dw_down)
+    return carry, (*dw_heads, dw_out[None], dw_up, dw_down)
 
 
 def stack_grads(grads_by_layer):

time: 466 us -> 433 us (0.929)
  Pallas kernels: 458 us -> 432 us
    pallas_call x2, Pallas kernels: 356 us -> 329 us  [run_exchange(): pl.pallas_call(functools.partial(exchange_kernel, side, tuple(row_arrays)...]
where the time goes in v3:
time: 433 us
  Pallas kernels  432 us (100%)
    pallas_call x2, Pallas kernels, run_exchange(): pl.pallas_call(functools.partial(exchange_kernel, side, tuple(row_arrays)...  329 us
    pallas_call x1, Pallas kernels, run_attn(): pl.pallas_call(functools.partial(attn_kernel, seq_tok, group), grid=(n_to...  42.9 us
    pallas_call x1, Pallas kernels, run_ffn(): pl.pallas_call(ffn_kernel, grid=(n_tok // tile,), in_specs=[rows, rows, w...  35.4 us
    pallas_call x1, Pallas kernels, run_widen(): pl.pallas_call(widen_kernel, grid=(n_tok // tile,), in_specs=[rows, rows]...  25.1 us

profile of v3, /device:TPU:97, one launch (start us, length us, event | category | flops | bytes accessed | tf_op | source)
XLA Modules:
  0.0 432.7 jit_solution(6900975636853233745)
XLA Ops:
  0.6 35.4 %ffn.1 = (f32[3072,2048]{1,0:T(8,128)}, bf16[3072,2048]{1,0:T(8,128)(2,1)}, f32[256,2048]{1,0:T(8,128)}, f32[256,2048]{1,0:T(8,128)}) custom-call(f32[3072,2048]{1,0:T(8,128)} %bitcast.42, f32[3072,2048]{1,0:T(8,128)} %bitcast.48, bf16[2048,256]{1,0:T(8,128)(2,1)} %bitcast.59, bf16[256,2048]{1,0:T(8,128)(2,1)} %bitcast.60), custom_call_target="tpu_custom_call" | custom-call | flops 19327352832 | bytes 88080384 | tf_op jit(solution)/shard_map/ffn/pallas_call | solution.py:374
  36.1 184.2 %exchange_g.1 = (bf16[4,4,2,96,2048]{4,3,2,1,0:T(8,128)(2,1)}, bf16[4,4,2,96,2176]{4,3,2,1,0:T(8,128)(2,1)}, f32[96,2048]{1,0:T(8,128)}) custom-call(bf16[4,4,2,96,2048]{4,3,2,1,0:T(8,128)(2,1)} %bitcast.52, f32[4,4,2,96,2048]{4,3,2,1,0:T(8,128)} %bitcast.47, f32[4,4,2,96,2048]{4,3,2,1,0:T(8,128)} %bitcast.43, f32[4,4,2,96,2048]{4,3,2,1,0:T(8,128)} %bitcast.45, ...), custom_call_target="tpu_custom_call" | custom-call | tf_op jit(solution)/shard_map/exchange_g/pallas_call | solution.py:455
  220.3 42.9 %attn.1 = (f32[3072,2048]{1,0:T(8,128)}, f32[3072,2048]{1,0:T(8,128)}, bf16[3072,2048]{1,0:T(8,128)(2,1)}, bf16[3072,2048]{1,0:T(8,128)(2,1)}, f32[64,2048]{1,0:...) custom-call(bf16[3072,2176]{1,0:T(8,128)(2,1)} %bitcast.57, ...), custom_call_target="tpu_custom_call" | custom-call | flops 9663676416 | bytes 100663296 | tf_op jit(solution)/shard_map/attn/pallas_call | solution.py:396
  263.2 144.4 %exchange_f.1 = (bf16[4,4,2,96,2048]{4,3,2,1,0:T(8,128)(2,1)}, bf16[4,4,2,96,2048]{4,3,2,1,0:T(8,128)(2,1)}) custom-call(bf16[4,4,2,96,2048]{4,3,2,1,0:T(8,128)(2,1)} %bitcast.50, bf16[4,4,2,96,2048]{4,3,2,1,0:T(8,128)(2,1)} %bitcast.51, f32[4,4,2,96,2048]{4,3,2,1,0:T(8,128)} %bitcast.44, f32[4,4,2,96,2048]{4,3,2,1,0:T(8,128)} %bitcast.49, ...), custom_call_target="tpu_custom_call" | custom-call | tf_op jit(solution)/shard_map/exchange_f/pallas_call | solution.py:455
  407.6 25.1 %widen.1 = (f32[3072,2048]{1,0:T(8,128)}, f32[3072,2048]{1,0:T(8,128)}) custom-call(bf16[3072,2048]{1,0:T(8,128)(2,1)} %bitcast.53, bf16[3072,2048]{1,0:T(8,128)(2,1)} %bitcast.54), custom_call_target="tpu_custom_call" | custom-call | flops 6291456 | bytes 75497472 | tf_op jit(solution)/shard_map/widen/pallas_call | solution.py:417

commit v4 on v3

--- a/solution.py
+++ b/solution.py
@@ -53,14 +53,14 @@
     dy_b = dy_ref[...].astype(BF16)
     act_val, slope = gelu_and_slope(dot(norm_b, up_ref[...]))
     act_b = act_val.astype(BF16)
-    branch_ref[...] = dot(act_b, down_ref[...])
+    branch_ref[...] = dot(act_b, down_ref[...]).astype(BF16)
     d_pre = (slope * dot(dy_b, down_t[...])).astype(BF16)
     dnorm_ref[...] = dot(d_pre, up_t[...]).astype(BF16)
     ddown_ref[...] += dot(act_b, dy_b, TN)
     dup_ref[...] += dot(d_pre, norm_b, TN)
 
 
-def attn_kernel(seq_tok, group, nf_ref, dy_ref, lens_ref, query_ref, key_ref, value_ref, out_ref, dup_ref,
+def attn_kernel(seq_tok, group, n_rows, nf_ref, dy_ref, scale_ref, lens_ref, query_ref, key_ref, value_ref, out_ref, dup_ref,
                 x2_ref, dy1_ref, branch_ref, dnorm_ref, dq_ref, dk_ref, dv_ref, dout_ref, dup_t, qkv, qkv_t, out_t):
     head_dim = query_ref.shape[0]
     score_scale = head_dim ** -0.5
@@ -77,9 +77,14 @@
         dout_ref[...] = jnp.zeros_like(dout_ref)
         dup_t[...] = dup_ref[...].T
 
-    norm_b = nf_ref[:, :width]
-    scales = nf_ref[:, width:].astype(F32)
-    x2_ref[...] = norm_b.astype(F32) * (scales[:, :1] + scales[:, LANES // 2:LANES // 2 + 1])
+    norm_b = nf_ref[...]
+    row = lax.broadcasted_iota(jnp.int32, (n_rows, LANES), 0)
+    own_lane = lax.broadcasted_iota(jnp.int32, (n_rows, LANES), 1) == row
+    for block in range(n_tok // n_rows):
+        scales = scale_ref[block * 16:(block + 1) * 16].astype(F32)
+        scale = jnp.where(own_lane, scales[:1] + scales[1:2], 0.0)
+        at = slice(block * n_rows, (block + 1) * n_rows)
+        x2_ref[at] = norm_b[at].astype(F32) * jnp.sum(scale, axis=1, keepdims=True)
     dy_b = dy_ref[...]
     dy1_ref[...] = dy_b.astype(F32)
 
@@ -129,39 +134,48 @@
     dx2_ref[...] = dx2_in[...].astype(F32)
 
 
-def store_x2(total, rows, out, x2_out, at):
+def store_x2(total, rows, out, x2_out, scale_buf, at):
     x_two = rows['y_two'][at] - total[at]
     x2_out[at] = x_two
     normed, inv_rms = rms_norm(x_two)
-    width = normed.shape[1]
-    scale = jnp.broadcast_to(1.0 / inv_rms, (normed.shape[0], LANES))
+    out[at] = normed.astype(BF16)
+    scale_buf[at[0]] = jnp.broadcast_to(1.0 / inv_rms, (normed.shape[0], LANES))
+
+
+def pack_scales(scale_buf, out):
+    n_rows = scale_buf.shape[0]
+    row = lax.broadcasted_iota(jnp.int32, (n_rows, LANES), 0)
+    lane = lax.broadcasted_iota(jnp.int32, (n_rows, LANES), 1)
+    scale = jnp.sum(jnp.where(row == lane, scale_buf[...], 0.0), axis=0, keepdims=True)
     high = scale.astype(BF16).astype(F32)
-    lane = lax.broadcasted_iota(jnp.int32, scale.shape, 1)
-    out[at[0], :width] = normed.astype(BF16)
-    out[at[0], width:] = jnp.where(lane < LANES // 2, high, scale - high).astype(BF16)
-
-
-def store_dy1(total, rows, out, x2_out, at):
+    part = lax.broadcasted_iota(jnp.int32, out.shape, 0)
+    out[...] = jnp.where(part == 0, high, scale - high).astype(BF16)
+
+
+def store_dy1(total, rows, out, x2_out, scale_buf, at):
     out[at] = (rows['dy_one'][at] + rms_back(*rms_norm(rows['y_one'][at]), total[at])).astype(BF16)
 
 
-def store_x1(total, rows, out, x2_out, at):
+def store_x1(total, rows, out, x2_out, scale_buf, at):
     out[at] = (rows['y_one'][at] - total[at]).astype(BF16)
 
 
-def store_dx2(total, rows, out, x2_out, at):
+def store_dx2(total, rows, out, x2_out, scale_buf, at):
     out[at] = (rows['dy_two'][at] + rms_back(*rms_norm(rows['x_two'][at]), total[at])).astype(BF16)
 
 
 def exchange_kernel(side, row_names, stores, keeps_x2, *refs):
     n_row = len(row_names)
     parts, row_refs, refs = refs[:2], refs[2:2 + n_row], refs[2 + n_row:]
-    outs, refs = refs[:2], refs[2:]
-    x2_out = None
+    n_out = 3 if keeps_x2 else 2
+    outs, refs = refs[:n_out], refs[n_out:]
+    x2_out = scale_buf = None
     if keeps_x2:
         x2_out, refs = refs[0], refs[1:]
     paired, own, slot_a, slot_b, total, sent = (refs[2 * i:2 * i + 2] for i in range(6))
     refs = refs[12:]
+    if keeps_x2:
+        sent, scale_buf, refs = (*sent, refs[0]), refs[1], refs[2:]
     row_bufs, refs = dict(zip(row_names, refs[:n_row])), refs[n_row:]
     (pair_send, pair_recv, own_sem, a_send, a_recv, b_send, b_recv, row_sem, out_sem,
      c_send, c_recv, d_send, d_recv, e_send, e_recv) = refs
@@ -185,8 +199,10 @@
         return {'tp': (place['y'] * side + place['x']) * 2 + core}
 
     def cols(k, st):
-        stop = (st + 1) * quarter if st < 3 else outs[k].shape[-1]
-        return slice(st * quarter, stop)
+        return slice(st * quarter, (st + 1) * quarter) if k < 2 else slice(None)
+
+    def lanes(k):
+        return range(4 if k < 2 else 1)
 
     def line(ref, axis, block, *rest):
         return ref.at[(slice(None), block) + rest] if axis == 'x' else ref.at[(block, slice(None)) + rest]
@@ -317,25 +333,30 @@
                 @pl.loop(0, n_rows // 16)
                 def _(r, k=k):
                     at = (pl.ds(pl.multiple_of(r * 16, 16), 16), slice(0, width))
-                    stores[k](total[k], row_bufs, sent[k], x2_out, at)
-                out_copies.append(pltpu.make_async_copy(sent[k], outs[k].at[pos['y'], pos['x'], core], out_sem.at[k]))
-                out_copies[-1].start()
-                for st in range(4):
-                    going[k, st] = gather_b(k, st, 0)
+                    stores[k](total[k], row_bufs, sent[k], x2_out, scale_buf, at)
+                ready = [k]
+                if k == 1 and n_out == 3:
+                    pack_scales(scale_buf, sent[2])
+                    ready.append(2)
+                for i in ready:
+                    out_copies.append(pltpu.make_async_copy(sent[i], outs[i].at[pos['y'], pos['x'], core], out_sem.at[i]))
+                    out_copies[-1].start()
+                    for st in lanes(i):
+                        going[i, st] = gather_b(i, st, 0)
 
     for step in range(steps):
-        for k in range(2):
+        for k in range(n_out):
             if step + 1 == steps:
                 out_copies[k].wait()
-            for st in range(4):
+            for st in lanes(k):
                 going[k, st].wait_recv()
                 if step + 1 < steps:
                     going[k, st] = gather_b(k, st, step + 1)
                 else:
                     gather_a(k, st, 0)
     for step in range(steps):
-        for k in range(2):
-            for st in range(4):
+        for k in range(n_out):
+            for st in lanes(k):
                 going[k, st].wait_recv()
                 gather_a(k, st, step + 1)
     for copy in last:
@@ -368,7 +389,7 @@
 
 def run_ffn(y_one, dy_two, w_up, w_down):
     (n_tok, width), cols = y_one.shape, w_up.shape[1]
-    tile = tile_of(n_tok, 512)
+    tile = tile_of(n_tok, 256)
     rows = pl.BlockSpec((tile, width), lambda i: (i, 0))
     grad = pl.BlockSpec((cols, width), lambda i: (0, 0))
     return pl.pallas_call(
@@ -376,7 +397,7 @@
         grid=(n_tok // tile,),
         in_specs=[rows, rows, whole(w_up), whole(w_down)],
         out_specs=[rows, rows, grad, grad],
-        out_shape=[shape_of((n_tok, width)), shape_of((n_tok, width), BF16)] + [shape_of((cols, width))] * 2,
+        out_shape=[shape_of((n_tok, width), BF16)] * 2 + [shape_of((cols, width))] * 2,
         scratch_shapes=[pltpu.VMEM((cols, width), BF16), pltpu.VMEM((width, cols), BF16)],
         compiler_params=params(),
         cost_estimate=pl.CostEstimate(flops=12 * n_tok * width * cols, bytes_accessed=14 * n_tok * width,
@@ -385,18 +406,19 @@
     )(y_one, dy_two, w_up, w_down)
 
 
-def run_attn(seq_tok, norm_f, dy_one, seq_lens, w_heads, w_out, dw_up):
+def run_attn(seq_tok, norm_f, dy_one, scales, seq_lens, w_heads, w_out, dw_up):
     n_tok, width = dy_one.shape
     head_dim = w_out.shape[0]
-    tile = tile_of(n_tok, 256)
+    n_rows = n_tok * 16 // scales.shape[0]
+    tile = 4 * n_rows
     group = tile_of(tile, 128)
     rows = pl.BlockSpec((tile, width), lambda i: (i, 0))
     grads = [whole(w) for w in w_heads] + [whole(w_out)]
     up_shape = dw_up.shape[::-1]
     return pl.pallas_call(
-        functools.partial(attn_kernel, seq_tok, group),
+        functools.partial(attn_kernel, seq_tok, group, n_rows),
         grid=(n_tok // tile,),
-        in_specs=[pl.BlockSpec((tile, norm_f.shape[1]), lambda i: (i, 0)), rows,
+        in_specs=[rows, rows, pl.BlockSpec((tile // n_rows * 16, LANES), lambda i: (i, 0)),
                   pl.BlockSpec(memory_space=pltpu.SMEM)] + grads + [whole(dw_up)],
         out_specs=[rows, rows, rows, rows] + grads + [pl.BlockSpec(up_shape, lambda i: (0, 0))],
         out_shape=[shape_of((n_tok, width))] * 2 + [shape_of((n_tok, width), BF16)] * 2
@@ -407,12 +429,12 @@
         cost_estimate=pl.CostEstimate(flops=24 * n_tok * width * head_dim, bytes_accessed=16 * n_tok * width,
                                       transcendentals=n_tok * group),
         name='attn',
-    )(norm_f, dy_one, seq_lens, *w_heads, w_out, dw_up)
+    )(norm_f, dy_one, scales, seq_lens, *w_heads, w_out, dw_up)
 
 
 def run_widen(x_one, dx_two):
     n_tok, width = x_one.shape
-    tile = tile_of(n_tok, 384)
+    tile = tile_of(n_tok, 512)
     rows = pl.BlockSpec((tile, width), lambda i: (i, 0))
     return pl.pallas_call(
         widen_kernel,
@@ -426,7 +448,7 @@
     )(x_one, dx_two)
 
 
-def run_exchange(n_dev, call_id, parts, row_arrays, stores, out_widths, keeps_x2, name):
+def run_exchange(n_dev, call_id, parts, row_arrays, stores, keeps_x2, name):
     side = int(round((n_dev // 2) ** 0.5))
     n_tok, width = parts[0].shape
     n_rows = n_tok // n_dev
@@ -435,8 +457,9 @@
     def blocks(arr):
         return arr.reshape(side, side, 2, n_rows, arr.shape[1]) if arr.shape[0] == n_tok else arr
 
-    outs = [shape_of((side, side, 2, n_rows, w), BF16) for w in out_widths]
-    out_specs = [ANY] * 2
+    sent = [(n_rows, width)] * 2 + ([(16, LANES)] if keeps_x2 else [])
+    outs = [shape_of((side, side, 2) + dims, BF16) for dims in sent]
+    out_specs = [ANY] * len(outs)
     if keeps_x2:
         outs.append(shape_of((n_rows, width)))
         out_specs.append(pl.BlockSpec(memory_space=pltpu.VMEM))
@@ -446,12 +469,14 @@
     scratch += [pltpu.VMEM((4, side - 1, side, n_rows, quarter), kind) for kind in kinds]
     scratch += [pltpu.VMEM((4, side - 1, n_rows, quarter), kind) for kind in kinds]
     scratch += [pltpu.VMEM((n_rows, width), F32)] * 2
-    scratch += [pltpu.VMEM((n_rows, w), BF16) for w in out_widths]
+    scratch += [pltpu.VMEM(dims, BF16) for dims in sent]
+    if keeps_x2:
+        scratch.append(pltpu.VMEM((n_rows, LANES), F32))
     scratch += [pltpu.VMEM((n_rows, width), F32)] * len(row_arrays)
     dma = pltpu.SemaphoreType.DMA
-    ring = dma((2, 4, side - 1))
-    scratch += [dma((2, 4, side))] * 2 + [dma((2, 4))] + [ring] * 4 + [dma((len(row_arrays),)), dma((2,))]
-    scratch += [ring] * 4 + [dma((2, 4, side))] * 2
+    ring, gather_ring = dma((2, 4, side - 1)), dma((3, 4, side - 1))
+    scratch += [dma((2, 4, side))] * 2 + [dma((2, 4))] + [ring] * 4 + [dma((len(row_arrays),)), dma((3,))]
+    scratch += [gather_ring] * 4 + [dma((3, 4, side))] * 2
     gathered = pl.pallas_call(
         functools.partial(exchange_kernel, side, tuple(row_arrays), stores, keeps_x2),
         in_specs=[ANY] * (2 + len(row_arrays)),
@@ -473,14 +498,14 @@
     w_heads = [w[:, 0, :].T for w in (w_query, w_key, w_value)]
 
     g_part, dg_part, dw_up, dw_down = run_ffn(y_one, dy_two, w_up, w_down)
-    dy1_b, norm_f, x2_rows = run_exchange(
+    dy1_b, norm_f, scales, x2_rows = run_exchange(
         n_dev, 0, (dg_part, g_part), {'y_one': y_one, 'y_two': y_two, 'dy_one': dy_one},
-        (store_dy1, store_x2), (width, width + LANES), True, 'exchange_g')
+        (store_dy1, store_x2), True, 'exchange_g')
     x_two, dy_one, f_part, df_part, *dw_heads, dw_out, dw_up = run_attn(
-        seq_tok, norm_f, dy1_b, seq_lens, w_heads, w_out[0], dw_up)
+        seq_tok, norm_f, dy1_b, scales, seq_lens, w_heads, w_out[0], dw_up)
     x1_b, dx2_b = run_exchange(
         n_dev, 1, (f_part, df_part), {'y_one': y_one, 'dy_two': dy_two, 'x_two': x2_rows},
-        (store_x1, store_dx2), (width, width), False, 'exchange_f')
+        (store_x1, store_dx2), False, 'exchange_f')
     x_one, dx_two = run_widen(x1_b, dx2_b)
     dw_heads = [dw.T[:, None, :] for dw in dw_heads]
     carry = tuple(a.reshape(act_shape) for a in (x_one, x_two, dy_one, dx_two))

time: 433 us -> 399 us (0.921)
  Pallas kernels: 432 us -> 398 us
    pallas_call x2, Pallas kernels: 329 us -> 296 us  [run_exchange(): pl.pallas_call(functools.partial(exchange_kernel, side, tuple(row_arrays)...]
where the time goes in v4:
time: 399 us
  Pallas kernels  398 us (100%)
    pallas_call x2, Pallas kernels, run_exchange(): pl.pallas_call(functools.partial(exchange_kernel, side, tuple(row_arrays)...  296 us
    pallas_call x1, Pallas kernels, run_attn(): pl.pallas_call(functools.partial(attn_kernel, seq_tok, group, n_rows), gr...  41.3 us
    pallas_call x1, Pallas kernels, run_ffn(): pl.pallas_call(ffn_kernel, grid=(n_tok // tile,), in_specs=[rows, rows, w...  36.5 us
    pallas_call x1, Pallas kernels, run_widen(): pl.pallas_call(widen_kernel, grid=(n_tok // tile,), in_specs=[rows, rows]...  23.9 us

profile of v4, /device:TPU:97, one launch (start us, length us, event | category | flops | bytes accessed | tf_op | source)
XLA Modules:
  0.0 398.5 jit_solution(7233012101243443109)
XLA Ops:
  0.6 36.5 %ffn.1 = (bf16[3072,2048]{1,0:T(8,128)(2,1)}, bf16[3072,2048]{1,0:T(8,128)(2,1)}, f32[256,2048]{1,0:T(8,128)}, f32[256,2048]{1,0:T(8,128)}) custom-call(f32[3072,2048]{1,0:T(8,128)} %bitcast.43, f32[3072,2048]{1,0:T(8,128)} %bitcast.48, bf16[2048,256]{1,0:T(8,128)(2,1)} %bitcast.60, bf16[256,2048]{1,0:T(8,128)(2,1)} %bitcast.61), custom_call_target="tpu_custom_call" | custom-call | flops 19327352832 | bytes 88080384 | tf_op jit(solution)/shard_map/ffn/pallas_call | solution.py:395
  37.1 151.9 %exchange_g.1 = (bf16[4,4,2,96,2048]{4,3,2,1,0:T(8,128)(2,1)}, bf16[4,4,2,96,2048]{4,3,2,1,0:T(8,128)(2,1)}, bf16[4,4,2,16,128]{4,3,2,1,0:T(8,128)(2,1)}, f32[96,2048]{1,0:T(8,128)}) custom-call(bf16[4,4,2,96,2048]{4,3,2,1,0:T(8,128)(2,1)} %bitcast.53, bf16[4,4,2,96,2048]{4,3,2,1,0:T(8,128)(2,1)} %bitcast.52, f32[4,4,2,96,2048]{4,3,2,1,0:T(8,128)} %bitcast.44, ...), custom_call_target="tpu_custom_call" | custom-call | tf_op jit(solution)/shard_map/exchange_g/pallas_call | solution.py:480
  189.1 41.3 %attn.1 = (f32[3072,2048]{1,0:T(8,128)}, f32[3072,2048]{1,0:T(8,128)}, bf16[3072,2048]{1,0:T(8,128)(2,1)}, bf16[3072,2048]{1,0:T(8,128)(2,1)}, f32[64,2048]{1,0:...) custom-call(bf16[3072,2048]{1,0:T(8,128)(2,1)} %bitcast.59, ...), custom_call_target="tpu_custom_call" | custom-call | flops 9663676416 | bytes 100663296 | tf_op jit(solution)/shard_map/attn/pallas_call | solution.py:418
  230.4 144.2 %exchange_f.1 = (bf16[4,4,2,96,2048]{4,3,2,1,0:T(8,128)(2,1)}, bf16[4,4,2,96,2048]{4,3,2,1,0:T(8,128)(2,1)}) custom-call(bf16[4,4,2,96,2048]{4,3,2,1,0:T(8,128)(2,1)} %bitcast.50, bf16[4,4,2,96,2048]{4,3,2,1,0:T(8,128)(2,1)} %bitcast.51, f32[4,4,2,96,2048]{4,3,2,1,0:T(8,128)} %bitcast.45, f32[4,4,2,96,2048]{4,3,2,1,0:T(8,128)} %bitcast.49, ...), custom_call_target="tpu_custom_call" | custom-call | tf_op jit(solution)/shard_map/exchange_f/pallas_call | solution.py:480
  374.6 23.9 %widen.1 = (f32[3072,2048]{1,0:T(8,128)}, f32[3072,2048]{1,0:T(8,128)}) custom-call(bf16[3072,2048]{1,0:T(8,128)(2,1)} %bitcast.54, bf16[3072,2048]{1,0:T(8,128)(2,1)} %bitcast.55), custom_call_target="tpu_custom_call" | custom-call | flops 6291456 | bytes 75497472 | tf_op jit(solution)/shard_map/widen/pallas_call | solution.py:439

commit v5 on v4

--- a/solution.py
+++ b/solution.py
@@ -134,34 +134,34 @@
     dx2_ref[...] = dx2_in[...].astype(F32)
 
 
-def store_x2(total, rows, out, x2_out, scale_buf, at):
+def store_x2(total, rows, x2_out, scale_buf, at):
     x_two = rows['y_two'][at] - total[at]
     x2_out[at] = x_two
     normed, inv_rms = rms_norm(x_two)
-    out[at] = normed.astype(BF16)
     scale_buf[at[0]] = jnp.broadcast_to(1.0 / inv_rms, (normed.shape[0], LANES))
-
-
-def pack_scales(scale_buf, out):
+    return normed.astype(BF16)
+
+
+def pack_scales(scale_buf, shape):
     n_rows = scale_buf.shape[0]
     row = lax.broadcasted_iota(jnp.int32, (n_rows, LANES), 0)
     lane = lax.broadcasted_iota(jnp.int32, (n_rows, LANES), 1)
     scale = jnp.sum(jnp.where(row == lane, scale_buf[...], 0.0), axis=0, keepdims=True)
     high = scale.astype(BF16).astype(F32)
-    part = lax.broadcasted_iota(jnp.int32, out.shape, 0)
-    out[...] = jnp.where(part == 0, high, scale - high).astype(BF16)
-
-
-def store_dy1(total, rows, out, x2_out, scale_buf, at):
-    out[at] = (rows['dy_one'][at] + rms_back(*rms_norm(rows['y_one'][at]), total[at])).astype(BF16)
-
-
-def store_x1(total, rows, out, x2_out, scale_buf, at):
-    out[at] = (rows['y_one'][at] - total[at]).astype(BF16)
-
-
-def store_dx2(total, rows, out, x2_out, scale_buf, at):
-    out[at] = (rows['dy_two'][at] + rms_back(*rms_norm(rows['x_two'][at]), total[at])).astype(BF16)
+    part = lax.broadcasted_iota(jnp.int32, shape, 0)
+    return jnp.where(part == 0, high, scale - high).astype(BF16)
+
+
+def store_dy1(total, rows, x2_out, scale_buf, at):
+    return (rows['dy_one'][at] + rms_back(*rms_norm(rows['y_one'][at]), total[at])).astype(BF16)
+
+
+def store_x1(total, rows, x2_out, scale_buf, at):
+    return (rows['y_one'][at] - total[at]).astype(BF16)
+
+
+def store_dx2(total, rows, x2_out, scale_buf, at):
+    return (rows['dy_two'][at] + rms_back(*rms_norm(rows['x_two'][at]), total[at])).astype(BF16)
 
 
 def exchange_kernel(side, row_names, stores, keeps_x2, *refs):
@@ -172,10 +172,10 @@
     x2_out = scale_buf = None
     if keeps_x2:
         x2_out, refs = refs[0], refs[1:]
-    paired, own, slot_a, slot_b, total, sent = (refs[2 * i:2 * i + 2] for i in range(6))
-    refs = refs[12:]
+    paired, own, slot_a, slot_b, sums, total, held = (refs[2 * i:2 * i + 2] for i in range(7))
+    refs = refs[14:]
     if keeps_x2:
-        sent, scale_buf, refs = (*sent, refs[0]), refs[1], refs[2:]
+        held, scale_buf, refs = (*held, refs[0]), refs[1], refs[2:]
     row_bufs, refs = dict(zip(row_names, refs[:n_row])), refs[n_row:]
     (pair_send, pair_recv, own_sem, a_send, a_recv, b_send, b_recv, row_sem, out_sem,
      c_send, c_recv, d_send, d_recv, e_send, e_recv) = refs
@@ -282,7 +282,10 @@
                 def _(j, k=k, st=st, turn=turn):
                     mine = paired[k][st, turn, j].astype(F32) + own[k][st, j].astype(F32)
                     if turn:
-                        slot_a[k][st, turn - 1, j] = (slot_a[k][st, turn - 1, j].astype(F32) + mine).astype(slot_a[k].dtype)
+                        mine += slot_a[k][st, turn - 1, j].astype(F32)
+                        slot_a[k][st, turn - 1, j] = mine.astype(slot_a[k].dtype)
+                        if turn == steps:
+                            sums[k][st, j] = mine
                     else:
                         paired[k][st, 0, j] = mine.astype(paired[k].dtype)
 
@@ -296,11 +299,8 @@
     def gather_b(k, st, step):
         axis, sign = streams[st]
         axis = other[axis]
-        at = dict(pos)
-        at[axis] = wrap(pos[axis] - sign * step)
-        block = outs[k].at[at['y'], at['x'], core, :, cols(k, st)]
-        src = sent[k].at[:, cols(k, st)] if step == 0 else block
-        copy = remote(src, block, c_send.at[k, st, step], c_recv.at[k, st, step], device(axis, sign))
+        block = held[k].at[st, wrap(pos[axis] - sign * step)]
+        copy = remote(block, block, c_send.at[k, st, step], c_recv.at[k, st, step], device(axis, sign))
         copy.start()
         waits.append(copy)
         return copy
@@ -308,46 +308,49 @@
     def gather_a(k, st, step):
         axis, sign = streams[st]
         group = line(outs[k], axis, wrap(pos[axis] - sign * step), core, slice(None), cols(k, st))
+        src = held[k].at[st] if step == 0 else group
         if step < steps:
-            copy = remote(group, group, d_send.at[k, st, step], d_recv.at[k, st, step], device(axis, sign))
+            copy = remote(src, group, d_send.at[k, st, step], d_recv.at[k, st, step], device(axis, sign))
             copy.start()
             waits.append(copy)
             going[k, st] = copy
-        copy = remote(group, group, e_send.at[k, st, step], e_recv.at[k, st, step], {'tp': partner})
+        copy = remote(src, group, e_send.at[k, st, step], e_recv.at[k, st, step], {'tp': partner})
         copy.start()
         waits.append(copy)
         last.append(copy)
+        if step == 0:
+            copy = pltpu.make_async_copy(src, group, out_sem.at[k, st])
+            copy.start()
+            out_copies.append(copy)
 
     last, out_copies = [], []
     for step in range(steps):
         for k in range(2):
             for st, (axis, sign) in enumerate(streams):
                 going[k, st].wait_recv()
-                mine = slot_a[k].at[st, steps - 1, wrap(pos[other[axis]] - sign * (2 + step))]
+                mine = sums[k].at[st, wrap(pos[other[axis]] - sign * (2 + step))]
                 if step + 1 < steps:
-                    slot_b[k][st, step] = (slot_b[k][st, step].astype(F32) + mine[...].astype(F32)).astype(slot_b[k].dtype)
+                    slot_b[k][st, step] = (slot_b[k][st, step].astype(F32) + mine[...]).astype(slot_b[k].dtype)
                     going[k, st] = send_b(k, st, step + 1)
                 else:
-                    total[k][:, st * quarter:(st + 1) * quarter] = slot_b[k][st, step].astype(F32) + mine[...].astype(F32)
+                    total[k][:, st * quarter:(st + 1) * quarter] = slot_b[k][st, step].astype(F32) + mine[...]
             if step + 1 == steps:
                 @pl.loop(0, n_rows // 16)
                 def _(r, k=k):
                     at = (pl.ds(pl.multiple_of(r * 16, 16), 16), slice(0, width))
-                    stores[k](total[k], row_bufs, sent[k], x2_out, scale_buf, at)
+                    vals = stores[k](total[k], row_bufs, x2_out, scale_buf, at)
+                    for st, (axis, sign) in enumerate(streams):
+                        held[k][st, pos[other[axis]], at[0]] = vals[:, cols(k, st)]
                 ready = [k]
                 if k == 1 and n_out == 3:
-                    pack_scales(scale_buf, sent[2])
+                    held[2][0, pos['y']] = pack_scales(scale_buf, held[2].shape[2:])
                     ready.append(2)
                 for i in ready:
-                    out_copies.append(pltpu.make_async_copy(sent[i], outs[i].at[pos['y'], pos['x'], core], out_sem.at[i]))
-                    out_copies[-1].start()
                     for st in lanes(i):
                         going[i, st] = gather_b(i, st, 0)
 
     for step in range(steps):
         for k in range(n_out):
-            if step + 1 == steps:
-                out_copies[k].wait()
             for st in lanes(k):
                 going[k, st].wait_recv()
                 if step + 1 < steps:
@@ -359,6 +362,8 @@
             for st in lanes(k):
                 going[k, st].wait_recv()
                 gather_a(k, st, step + 1)
+    for copy in out_copies:
+        copy.wait()
     for copy in last:
         copy.wait_recv()
     for copy in waits:
@@ -389,7 +394,7 @@
 
 def run_ffn(y_one, dy_two, w_up, w_down):
     (n_tok, width), cols = y_one.shape, w_up.shape[1]
-    tile = tile_of(n_tok, 256)
+    tile = tile_of(n_tok, 512)
     rows = pl.BlockSpec((tile, width), lambda i: (i, 0))
     grad = pl.BlockSpec((cols, width), lambda i: (0, 0))
     return pl.pallas_call(
@@ -434,7 +439,7 @@
 
 def run_widen(x_one, dx_two):
     n_tok, width = x_one.shape
-    tile = tile_of(n_tok, 512)
+    tile = tile_of(n_tok, 768)
     rows = pl.BlockSpec((tile, width), lambda i: (i, 0))
     return pl.pallas_call(
         widen_kernel,
@@ -468,14 +473,15 @@
     scratch += [pltpu.VMEM((4, side, n_rows, quarter), kind) for kind in kinds]
     scratch += [pltpu.VMEM((4, side - 1, side, n_rows, quarter), kind) for kind in kinds]
     scratch += [pltpu.VMEM((4, side - 1, n_rows, quarter), kind) for kind in kinds]
+    scratch += [pltpu.VMEM((4, side, n_rows, quarter), F32)] * 2
     scratch += [pltpu.VMEM((n_rows, width), F32)] * 2
-    scratch += [pltpu.VMEM(dims, BF16) for dims in sent]
+    scratch += [pltpu.VMEM((4, side, n_rows, quarter), BF16)] * 2
     if keeps_x2:
-        scratch.append(pltpu.VMEM((n_rows, LANES), F32))
+        scratch += [pltpu.VMEM((1, side, 16, LANES), BF16), pltpu.VMEM((n_rows, LANES), F32)]
     scratch += [pltpu.VMEM((n_rows, width), F32)] * len(row_arrays)
     dma = pltpu.SemaphoreType.DMA
     ring, gather_ring = dma((2, 4, side - 1)), dma((3, 4, side - 1))
-    scratch += [dma((2, 4, side))] * 2 + [dma((2, 4))] + [ring] * 4 + [dma((len(row_arrays),)), dma((3,))]
+    scratch += [dma((2, 4, side))] * 2 + [dma((2, 4))] + [ring] * 4 + [dma((len(row_arrays),)), dma((3, 4))]
     scratch += [gather_ring] * 4 + [dma((3, 4, side))] * 2
     gathered = pl.pallas_call(
         functools.partial(exchange_kernel, side, tuple(row_arrays), stores, keeps_x2),

time: 399 us -> 396 us (level)
  no operation moved by 1% of the time
where the time goes in v5:
time: 396 us
  Pallas kernels  396 us (100%)
    pallas_call x2, Pallas kernels, run_exchange(): pl.pallas_call(functools.partial(exchange_kernel, side, tuple(row_arrays)...  296 us
    pallas_call x1, Pallas kernels, run_attn(): pl.pallas_call(functools.partial(attn_kernel, seq_tok, group, n_rows), gr...  41.3 us
    pallas_call x1, Pallas kernels, run_ffn(): pl.pallas_call(ffn_kernel, grid=(n_tok // tile,), in_specs=[rows, rows, w...  35.2 us
    pallas_call x1, Pallas kernels, run_widen(): pl.pallas_call(widen_kernel, grid=(n_tok // tile,), in_specs=[rows, rows]...  23.4 us

profile of v5, /device:TPU:97, one launch (start us, length us, event | category | flops | bytes accessed | tf_op | source)
XLA Modules:
  0.0 396.3 jit_solution(16794722378457917671)
XLA Ops:
  0.6 35.2 %ffn.1 = (bf16[3072,2048]{1,0:T(8,128)(2,1)}, bf16[3072,2048]{1,0:T(8,128)(2,1)}, f32[256,2048]{1,0:T(8,128)}, f32[256,2048]{1,0:T(8,128)}) custom-call(f32[3072,2048]{1,0:T(8,128)} %bitcast.43, f32[3072,2048]{1,0:T(8,128)} %bitcast.48, bf16[2048,256]{1,0:T(8,128)(2,1)} %bitcast.60, bf16[256,2048]{1,0:T(8,128)(2,1)} %bitcast.61), custom_call_target="tpu_custom_call" | custom-call | flops 19327352832 | bytes 88080384 | tf_op jit(solution)/shard_map/ffn/pallas_call | solution.py:400
  35.9 151.9 %exchange_g.1 = (bf16[4,4,2,96,2048]{4,3,2,1,0:T(8,128)(2,1)}, bf16[4,4,2,96,2048]{4,3,2,1,0:T(8,128)(2,1)}, bf16[4,4,2,16,128]{4,3,2,1,0:T(8,128)(2,1)}, f32[96,2048]{1,0:T(8,128)}) custom-call(bf16[4,4,2,96,2048]{4,3,2,1,0:T(8,128)(2,1)} %bitcast.53, bf16[4,4,2,96,2048]{4,3,2,1,0:T(8,128)(2,1)} %bitcast.52, f32[4,4,2,96,2048]{4,3,2,1,0:T(8,128)} %bitcast.44, ...), custom_call_target="tpu_custom_call" | custom-call | tf_op jit(solution)/shard_map/exchange_g/pallas_call | solution.py:486
  187.7 41.3 %attn.1 = (f32[3072,2048]{1,0:T(8,128)}, f32[3072,2048]{1,0:T(8,128)}, bf16[3072,2048]{1,0:T(8,128)(2,1)}, bf16[3072,2048]{1,0:T(8,128)(2,1)}, f32[64,2048]{1,0:...) custom-call(bf16[3072,2048]{1,0:T(8,128)(2,1)} %bitcast.59, ...), custom_call_target="tpu_custom_call" | custom-call | flops 9663676416 | bytes 100663296 | tf_op jit(solution)/shard_map/attn/pallas_call | solution.py:423
  229.1 143.9 %exchange_f.1 = (bf16[4,4,2,96,2048]{4,3,2,1,0:T(8,128)(2,1)}, bf16[4,4,2,96,2048]{4,3,2,1,0:T(8,128)(2,1)}) custom-call(bf16[4,4,2,96,2048]{4,3,2,1,0:T(8,128)(2,1)} %bitcast.50, bf16[4,4,2,96,2048]{4,3,2,1,0:T(8,128)(2,1)} %bitcast.51, f32[4,4,2,96,2048]{4,3,2,1,0:T(8,128)} %bitcast.45, f32[4,4,2,96,2048]{4,3,2,1,0:T(8,128)} %bitcast.49, ...), custom_call_target="tpu_custom_call" | custom-call | tf_op jit(solution)/shard_map/exchange_f/pallas_call | solution.py:486
  372.9 23.4 %widen.1 = (f32[3072,2048]{1,0:T(8,128)}, f32[3072,2048]{1,0:T(8,128)}) custom-call(bf16[3072,2048]{1,0:T(8,128)(2,1)} %bitcast.54, bf16[3072,2048]{1,0:T(8,128)(2,1)} %bitcast.55), custom_call_target="tpu_custom_call" | custom-call | flops 6291456 | bytes 75497472 | tf_op jit(solution)/shard_map/widen/pallas_call | solution.py:444

commit v6 on v5

--- a/solution.py
+++ b/solution.py
@@ -172,8 +172,8 @@
     x2_out = scale_buf = None
     if keeps_x2:
         x2_out, refs = refs[0], refs[1:]
-    paired, own, slot_a, slot_b, sums, total, held = (refs[2 * i:2 * i + 2] for i in range(7))
-    refs = refs[14:]
+    paired, own, slot_a, slot_b, sums, held = (refs[4 * i:4 * i + 4] for i in range(6))
+    total, refs = refs[24:26], refs[26:]
     if keeps_x2:
         held, scale_buf, refs = (*held, refs[0]), refs[1], refs[2:]
     row_bufs, refs = dict(zip(row_names, refs[:n_row])), refs[n_row:]
@@ -181,7 +181,9 @@
      c_send, c_recv, d_send, d_recv, e_send, e_recv) = refs
     steps = side - 1
     n_rows, width = total[0].shape
-    quarter = width // 4
+    quarter = width // 8
+    units = range(4)
+    n_unit = 4 + n_out - 2
 
     me = lax.axis_index('tp')
     core = me % 2
@@ -199,10 +201,11 @@
         return {'tp': (place['y'] * side + place['x']) * 2 + core}
 
     def cols(k, st):
-        return slice(st * quarter, (st + 1) * quarter) if k < 2 else slice(None)
+        start = (k % 2 * 4 + st) * quarter
+        return slice(start, start + quarter) if k < 4 else slice(None)
 
     def lanes(k):
-        return range(4 if k < 2 else 1)
+        return range(4 if k < 4 else 1)
 
     def line(ref, axis, block, *rest):
         return ref.at[(slice(None), block) + rest] if axis == 'x' else ref.at[(block, slice(None)) + rest]
@@ -224,13 +227,12 @@
 
     def piece(k, st, turn, whose):
         axis, sign = streams[st]
-        return line(parts[k], axis, wrap(pos[axis] - sign * (1 + turn)), whose, slice(None),
-                    slice(st * quarter, (st + 1) * quarter))
+        return line(parts[k // 2], axis, wrap(pos[axis] - sign * (1 + turn)), whose, slice(None), cols(k, st))
 
     def own_copy(k, st, turn):
         return pltpu.make_async_copy(piece(k, st, turn, core), own[k].at[st], own_sem.at[k, st])
 
-    for k in range(2):
+    for k in units:
         for st in range(4):
             own_copy(k, st, 0).start()
     pl.semaphore_wait(barrier, len(neighbours))
@@ -238,7 +240,7 @@
     waits = []
     pair = {}
     for turn in range(side):
-        for k in range(2):
+        for k in units:
             for st in range(4):
                 copy = remote(piece(k, st, turn, 1 - core), paired[k].at[st, turn], pair_send.at[k, st, turn],
                               pair_recv.at[k, st, turn], {'tp': partner})
@@ -271,7 +273,7 @@
 
     going = {}
     for turn in range(side):
-        for k in range(2):
+        for k in units:
             for st in range(4):
                 if turn:
                     going[k, st].wait_recv()
@@ -307,7 +309,7 @@
 
     def gather_a(k, st, step):
         axis, sign = streams[st]
-        group = line(outs[k], axis, wrap(pos[axis] - sign * step), core, slice(None), cols(k, st))
+        group = line(outs[k // 2], axis, wrap(pos[axis] - sign * step), core, slice(None), cols(k, st))
         src = held[k].at[st] if step == 0 else group
         if step < steps:
             copy = remote(src, group, d_send.at[k, st, step], d_recv.at[k, st, step], device(axis, sign))
@@ -325,7 +327,7 @@
 
     last, out_copies = [], []
     for step in range(steps):
-        for k in range(2):
+        for k in units:
             for st, (axis, sign) in enumerate(streams):
                 going[k, st].wait_recv()
                 mine = sums[k].at[st, wrap(pos[other[axis]] - sign * (2 + step))]
@@ -333,24 +335,25 @@
                     slot_b[k][st, step] = (slot_b[k][st, step].astype(F32) + mine[...]).astype(slot_b[k].dtype)
                     going[k, st] = send_b(k, st, step + 1)
                 else:
-                    total[k][:, st * quarter:(st + 1) * quarter] = slot_b[k][st, step].astype(F32) + mine[...]
-            if step + 1 == steps:
+                    total[k // 2][:, cols(k, st)] = slot_b[k][st, step].astype(F32) + mine[...]
+            if step + 1 == steps and k % 2:
                 @pl.loop(0, n_rows // 16)
                 def _(r, k=k):
                     at = (pl.ds(pl.multiple_of(r * 16, 16), 16), slice(0, width))
-                    vals = stores[k](total[k], row_bufs, x2_out, scale_buf, at)
+                    vals = stores[k // 2](total[k // 2], row_bufs, x2_out, scale_buf, at)
                     for st, (axis, sign) in enumerate(streams):
-                        held[k][st, pos[other[axis]], at[0]] = vals[:, cols(k, st)]
-                ready = [k]
-                if k == 1 and n_out == 3:
-                    held[2][0, pos['y']] = pack_scales(scale_buf, held[2].shape[2:])
-                    ready.append(2)
+                        for unit in (k - 1, k):
+                            held[unit][st, pos[other[axis]], at[0]] = vals[:, cols(unit, st)]
+                ready = [k - 1, k]
+                if k == 3 and n_out == 3:
+                    held[4][0, pos['y']] = pack_scales(scale_buf, held[4].shape[2:])
+                    ready.append(4)
                 for i in ready:
                     for st in lanes(i):
                         going[i, st] = gather_b(i, st, 0)
 
     for step in range(steps):
-        for k in range(n_out):
+        for k in range(n_unit):
             for st in lanes(k):
                 going[k, st].wait_recv()
                 if step + 1 < steps:
@@ -358,7 +361,7 @@
                 else:
                     gather_a(k, st, 0)
     for step in range(steps):
-        for k in range(n_out):
+        for k in range(n_unit):
             for st in lanes(k):
                 going[k, st].wait_recv()
                 gather_a(k, st, step + 1)
@@ -457,7 +460,7 @@
     side = int(round((n_dev // 2) ** 0.5))
     n_tok, width = parts[0].shape
     n_rows = n_tok // n_dev
-    quarter = width // 4
+    quarter = width // 8
 
     def blocks(arr):
         return arr.reshape(side, side, 2, n_rows, arr.shape[1]) if arr.shape[0] == n_tok else arr
@@ -468,21 +471,19 @@
     if keeps_x2:
         outs.append(shape_of((n_rows, width)))
         out_specs.append(pl.BlockSpec(memory_space=pltpu.VMEM))
-    kinds = [part.dtype for part in parts]
-    scratch = [pltpu.VMEM((4, side, side, n_rows, quarter), kind) for kind in kinds]
-    scratch += [pltpu.VMEM((4, side, n_rows, quarter), kind) for kind in kinds]
-    scratch += [pltpu.VMEM((4, side - 1, side, n_rows, quarter), kind) for kind in kinds]
-    scratch += [pltpu.VMEM((4, side - 1, n_rows, quarter), kind) for kind in kinds]
-    scratch += [pltpu.VMEM((4, side, n_rows, quarter), F32)] * 2
+    turns = (4, side, n_rows, quarter)
+    scratch = [pltpu.VMEM((4, side) + turns[1:], BF16)] * 4 + [pltpu.VMEM(turns, BF16)] * 4
+    scratch += [pltpu.VMEM((4, side - 1) + turns[1:], BF16)] * 4
+    scratch += [pltpu.VMEM((4, side - 1, n_rows, quarter), BF16)] * 4
+    scratch += [pltpu.VMEM(turns, F32)] * 4 + [pltpu.VMEM(turns, BF16)] * 4
     scratch += [pltpu.VMEM((n_rows, width), F32)] * 2
-    scratch += [pltpu.VMEM((4, side, n_rows, quarter), BF16)] * 2
     if keeps_x2:
         scratch += [pltpu.VMEM((1, side, 16, LANES), BF16), pltpu.VMEM((n_rows, LANES), F32)]
     scratch += [pltpu.VMEM((n_rows, width), F32)] * len(row_arrays)
     dma = pltpu.SemaphoreType.DMA
-    ring, gather_ring = dma((2, 4, side - 1)), dma((3, 4, side - 1))
-    scratch += [dma((2, 4, side))] * 2 + [dma((2, 4))] + [ring] * 4 + [dma((len(row_arrays),)), dma((3, 4))]
-    scratch += [gather_ring] * 4 + [dma((3, 4, side))] * 2
+    ring, gather_ring = dma((4, 4, side - 1)), dma((5, 4, side - 1))
+    scratch += [dma((4, 4, side))] * 2 + [dma((4, 4))] + [ring] * 4 + [dma((len(row_arrays),)), dma((5, 4))]
+    scratch += [gather_ring] * 4 + [dma((5, 4, side))] * 2
     gathered = pl.pallas_call(
         functools.partial(exchange_kernel, side, tuple(row_arrays), stores, keeps_x2),
         in_specs=[ANY] * (2 + len(row_arrays)),

time: 396 us -> 395 us (level)
  no operation moved by 1% of the time
where the time goes in v6:
time: 395 us
  Pallas kernels  394 us (100%)
    pallas_call x2, Pallas kernels, run_exchange(): pl.pallas_call(functools.partial(exchange_kernel, side, tuple(row_arrays)...  295 us
    pallas_call x1, Pallas kernels, run_attn(): pl.pallas_call(functools.partial(attn_kernel, seq_tok, group, n_rows), gr...  41.1 us
    pallas_call x1, Pallas kernels, run_ffn(): pl.pallas_call(ffn_kernel, grid=(n_tok // tile,), in_specs=[rows, rows, w...  35.2 us
    pallas_call x1, Pallas kernels, run_widen(): pl.pallas_call(widen_kernel, grid=(n_tok // tile,), in_specs=[rows, rows]...  23.4 us

profile of v6, /device:TPU:97, one launch (start us, length us, event | category | flops | bytes accessed | tf_op | source)
XLA Modules:
  0.0 394.9 jit_solution(6083124421626517520)
XLA Ops:
  0.6 35.2 %ffn.1 = (bf16[3072,2048]{1,0:T(8,128)(2,1)}, bf16[3072,2048]{1,0:T(8,128)(2,1)}, f32[256,2048]{1,0:T(8,128)}, f32[256,2048]{1,0:T(8,128)}) custom-call(f32[3072,2048]{1,0:T(8,128)} %bitcast.43, f32[3072,2048]{1,0:T(8,128)} %bitcast.48, bf16[2048,256]{1,0:T(8,128)(2,1)} %bitcast.60, bf16[256,2048]{1,0:T(8,128)(2,1)} %bitcast.61), custom_call_target="tpu_custom_call" | custom-call | flops 19327352832 | bytes 88080384 | tf_op jit(solution)/shard_map/ffn/pallas_call | solution.py:403
  35.9 151.4 %exchange_g.1 = (bf16[4,4,2,96,2048]{4,3,2,1,0:T(8,128)(2,1)}, bf16[4,4,2,96,2048]{4,3,2,1,0:T(8,128)(2,1)}, bf16[4,4,2,16,128]{4,3,2,1,0:T(8,128)(2,1)}, f32[96,2048]{1,0:T(8,128)}) custom-call(bf16[4,4,2,96,2048]{4,3,2,1,0:T(8,128)(2,1)} %bitcast.53, bf16[4,4,2,96,2048]{4,3,2,1,0:T(8,128)(2,1)} %bitcast.52, f32[4,4,2,96,2048]{4,3,2,1,0:T(8,128)} %bitcast.44, ...), custom_call_target="tpu_custom_call" | custom-call | tf_op jit(solution)/shard_map/exchange_g/pallas_call | solution.py:487
  187.2 41.1 %attn.1 = (f32[3072,2048]{1,0:T(8,128)}, f32[3072,2048]{1,0:T(8,128)}, bf16[3072,2048]{1,0:T(8,128)(2,1)}, bf16[3072,2048]{1,0:T(8,128)(2,1)}, f32[64,2048]{1,0:...) custom-call(bf16[3072,2048]{1,0:T(8,128)(2,1)} %bitcast.59, ...), custom_call_target="tpu_custom_call" | custom-call | flops 9663676416 | bytes 100663296 | tf_op jit(solution)/shard_map/attn/pallas_call | solution.py:426
  228.4 143.2 %exchange_f.1 = (bf16[4,4,2,96,2048]{4,3,2,1,0:T(8,128)(2,1)}, bf16[4,4,2,96,2048]{4,3,2,1,0:T(8,128)(2,1)}) custom-call(bf16[4,4,2,96,2048]{4,3,2,1,0:T(8,128)(2,1)} %bitcast.50, bf16[4,4,2,96,2048]{4,3,2,1,0:T(8,128)(2,1)} %bitcast.51, f32[4,4,2,96,2048]{4,3,2,1,0:T(8,128)} %bitcast.45, f32[4,4,2,96,2048]{4,3,2,1,0:T(8,128)} %bitcast.49, ...), custom_call_target="tpu_custom_call" | custom-call | tf_op jit(solution)/shard_map/exchange_f/pallas_call | solution.py:487
  371.5 23.4 %widen.1 = (f32[3072,2048]{1,0:T(8,128)}, f32[3072,2048]{1,0:T(8,128)}) custom-call(bf16[3072,2048]{1,0:T(8,128)(2,1)} %bitcast.54, bf16[3072,2048]{1,0:T(8,128)(2,1)} %bitcast.55), custom_call_target="tpu_custom_call" | custom-call | flops 6291456 | bytes 75497472 | tf_op jit(solution)/shard_map/widen/pallas_call | solution.py:447
